TPU v7x, 32 devices: a whole 2x2x4 slice. The times are simulated.
32 devices in a mesh: row: 8 (over z, core), col: 4 (over y, x).
Axes of the slice: x: 2, y: 2, z: 4, core: 2. Of those that a mesh axis runs over, the one named last changes fastest.
Arguments:
- velocity: float32 [1, 3, 64, 64, 256], P(None, None, 'row', 'col'), may hold values from -6 to 6
- tendency: float32 [1, 3, 64, 64, 256], P(None, None, 'row', 'col'), may hold values from -6 to 6
- step_size: float32 [1], replicated, may hold values from 0.1 to 0.6
- lift_weight: float32 [32, 3], replicated, may hold values from -3.5 to 3.5
- lift_bias: float32 [32], replicated, may hold values from -3 to 3
- spectral_weight: bfloat16 [2, 32, 32, 32, 1024], P(None, 'row', 'col'), may hold values from -6 to 6
- local_weight: float32 [32, 32], replicated, may hold values from -1 to 1
- local_bias: float32 [32], replicated, may hold values from -3 to 3
Outputs:
- features: bfloat16 [1, 32, 64, 64, 256], P(None, None, 'row', 'col')
All inputs are finite; a program needn't handle non-finite values.
Results may differ from a plain program's by a relative error of at most 0.001.
Values sent between devices are 32-bit elements; how exact they have to be, the bound alone decides.
A program may use at most 64 MiB of HBM per device.

v0:
```python
import functools
import math

import jax
import jax.numpy as jnp
import numpy as np
from jax import lax
from jax.experimental import pallas as pl
from jax.experimental.pallas import tpu as pltpu
from jax.sharding import PartitionSpec as P

KX = 32
KY = 32
KZ = 32
HIGHEST = lax.Precision.HIGHEST
F32 = jnp.float32
BF16 = jnp.bfloat16


def waves(count):
    index = np.arange(count)
    return np.where(index < count // 2, index, index - count)


def trig(wave, length):
    angle = ((wave[:, None] * np.arange(length)[None, :]) % length) * (2.0 * math.pi / length)
    return np.cos(angle), np.sin(angle)


def np_halves(table):
    table = np.asarray(table, np.float32)
    high = table.astype(jnp.bfloat16)
    low = (table - high.astype(np.float32)).astype(jnp.bfloat16)
    return high, low


def split(x):
    high = x.astype(BF16)
    return high, (x - high.astype(F32)).astype(BF16)


def dot(a, b):
    return jnp.dot(a, b, preferred_element_type=F32)


MESH = pl.DeviceIdType.MESH


def layer_kernel(
    kyl, kzl, part, scale, vel_ref, tend_ref, step_ref, zf_ref, yfh_ref, yfl_ref, w_ref, lift_ref, xf_ref, selc_ref,
    sels_ref, flag_ref, xb_ref, yh_ref, yl_ref, out_ref, w_vmem, wl_ref, zsend, zrecv, ypad, ysend, yrecv, m_ref, xsend, xrecv,
    lhs_ref, csend, w_sem, z_ss, z_rs, y_ss, y_rs, x_ss, x_rs, c_ss, c_rs,
):
    rows, cols = lax.axis_size("row"), lax.axis_size("col")
    my_row, my_col = lax.axis_index("row"), lax.axis_index("col")
    width_in, cells, _ = vel_ref.shape
    rk = zf_ref.shape[0] // cols
    a = ysend.shape[1] // kyl
    b = cells // a
    modes = kyl * kzl * KX
    chunks = xsend.shape[0]

    load = pltpu.make_async_copy(w_ref, w_vmem, w_sem)
    load.start()
    barrier = pltpu.get_barrier_semaphore()
    row_peers = [lax.rem(my_row + i, rows) for i in range(1, rows)]
    col_peers = [lax.rem(my_col + i, cols) for i in range(1, cols)]
    for peer in row_peers:
        pl.semaphore_signal(barrier, inc=1, device_id={"row": peer}, device_id_type=MESH)
    for peer in col_peers:
        pl.semaphore_signal(barrier, inc=1, device_id={"col": peer}, device_id_type=MESH)

    for j in range(width_in):
        adv = vel_ref[j] + step_ref[0] * tend_ref[j]
        z = lax.dot_general(
            zf_ref[...], adv, (((1,), (1,)), ((), ())), precision=HIGHEST, preferred_element_type=F32
        )
        zsend[:, j * rk:(j + 1) * rk, :] = z.reshape(cols, rk, cells)
    pl.semaphore_wait(barrier, rows + cols - 2)
    z_copies = []
    for i, peer in enumerate(col_peers):
        copy = pltpu.make_async_remote_copy(
            zsend.at[peer], zrecv.at[my_col], z_ss.at[i], z_rs.at[i], device_id={"col": peer}, device_id_type=MESH
        )
        copy.start()
        z_copies.append(copy)
    zrecv[pl.ds(my_col, 1)] = zsend[pl.ds(my_col, 1)]

    load.wait()
    step_rows = modes // 2
    half_lanes = lift_ref.shape[1] // 2

    def weigh(n):
        at = slice(n * step_rows, (n + 1) * step_rows)
        both = dot(w_vmem[at, :], lift_ref[...])
        wl_ref[at, :] = both[:, :half_lanes] + both[:, half_lanes:]

    weigh(0)
    weigh(1)
    for copy in z_copies:
        copy.wait_recv()

    x = jnp.concatenate([zrecv[s] for s in range(cols)], 1)
    xh, xl = split(x)
    y = dot(xh, yfh_ref[...]) + dot(xl, yfh_ref[...]) + dot(xh, yfl_ref[...])
    lanes = rows * kyl * a
    ypad[...] = jnp.zeros_like(ypad)
    low_rows = lax.broadcasted_iota(jnp.int32, (rk, lanes), 0) < rk // 2
    for j in range(width_in):
        block = y[j * rk:(j + 1) * rk]
        turned = pltpu.roll(block[:, lanes:], rk // 2, 0)
        ypad[j * rk:(j + 1) * rk, :] = block[:, :lanes] + jnp.where(low_rows, turned, -turned)
    ysend[...] = jnp.transpose(ypad[...]).reshape(ysend.shape)
    y_copies = []
    for i, peer in enumerate(row_peers):
        copy = pltpu.make_async_remote_copy(
            ysend.at[peer], yrecv.at[my_row], y_ss.at[i], y_rs.at[i], device_id={"row": peer}, device_id_type=MESH
        )
        copy.start()
        y_copies.append(copy)
    yrecv[pl.ds(my_row, 1)] = ysend[pl.ds(my_row, 1)]
    weigh(2)
    weigh(3)
    for copy in y_copies:
        copy.wait_recv()

    cos_parts, sin_parts = [], []
    for l in range(kyl):
        u = yrecv[:, l * a:(l + 1) * a, :].reshape(rows * a, yrecv.shape[2])
        q = jnp.dot(xf_ref[...], u, precision=HIGHEST, preferred_element_type=F32) * scale
        cos_parts.append(q[:KX])
        sin_parts.append(q[KX:])
    ch, cl = split(jnp.concatenate(cos_parts, 0))
    sh, sl = split(jnp.concatenate(sin_parts, 0))
    selc, sels = selc_ref[...], sels_ref[...]
    amp = dot(ch, selc) + dot(cl, selc) + dot(sh, sels) + dot(sl, sels)
    lane = lax.broadcasted_iota(jnp.int32, (KX, 128), 1)
    row = lax.broadcasted_iota(jnp.int32, (KX, 128), 0)
    quarter = lane // 32
    order = [(l, c * part + k) for c in range(chunks) for l in range(kyl) for k in range(part)]
    chunk_lanes = xsend.shape[3]
    x_copies = []
    for c in range(chunks):
        for group in range(chunk_lanes // 128):
            packed_r = packed_i = None
            for q in range(4):
                l, k = order[(c * chunk_lanes // 128 + group) * 4 + q]
                ar = amp[l * KX:(l + 1) * KX, k * 256:k * 256 + 128]
                ai = amp[l * KX:(l + 1) * KX, k * 256 + 128:k * 256 + 256]
                if l == 0 and k == 0:
                    ar = ar + jnp.where(row == 0, flag_ref[...], 0.0)
                at = (l * kzl + k) * KX
                wr = wl_ref[at:at + KX, :]
                wi = wl_ref[modes + at:modes + at + KX, :]
                pr = wr * ar - wi * ai
                pi = wr * ai + wi * ar
                pr = pr + pltpu.roll(pr, 64, 1)
                pi = pi + pltpu.roll(pi, 64, 1)
                pr = pr + pltpu.roll(pr, 32, 1)
                pi = pi + pltpu.roll(pi, 32, 1)
                packed_r = pr if q == 0 else jnp.where(quarter == q, pr, packed_r)
                packed_i = pi if q == 0 else jnp.where(quarter == q, pi, packed_i)
            at = slice(group * 128, (group + 1) * 128)
            mh, ml = split(jnp.concatenate([packed_r, packed_i], 0))
            m_ref[0:2 * KX, at] = mh
            m_ref[2 * KX:4 * KX, at] = ml
            m_ref[4 * KX:6 * KX, at] = mh
        xsend[c] = dot(xb_ref[...], m_ref[...]).reshape(xsend.shape[1:])
        started = []
        for i, peer in enumerate(row_peers):
            copy = pltpu.make_async_remote_copy(
                xsend.at[c, peer], xrecv.at[c, my_row], x_ss.at[c, i], x_rs.at[c, i],
                device_id={"row": peer}, device_id_type=MESH,
            )
            copy.start()
            started.append(copy)
        xrecv[c, pl.ds(my_row, 1)] = xsend[c, pl.ds(my_row, 1)]
        x_copies.append(started)

    total = rows * 2 * a
    ko = chunk_lanes // kyl
    pairs = 2 * rows
    width = 2 * cells
    xr = lax.broadcasted_iota(jnp.int32, (pairs, a, width), 1)
    xl = (lax.broadcasted_iota(jnp.int32, (pairs, a, width), 2) // b) % a
    same = xr == xl

    def expand(table):
        full = jnp.where(same, table.astype(F32)[:, None, :], 0.0)
        return full.reshape(total, width).astype(BF16)

    c_copies = []
    for c in range(chunks):
        for copy in x_copies[c]:
            copy.wait_recv()
        for l in range(kyl):
            held = xrecv[c, :, :, l * ko:(l + 1) * ko].reshape(total, ko)
            th, tl = split(jnp.transpose(held))
            lhs_ref[:, l * total:(l + 1) * total] = th
            lhs_ref[:, (kyl + l) * total:(kyl + l + 1) * total] = tl
            lhs_ref[:, (2 * kyl + l) * total:(2 * kyl + l + 1) * total] = th
        at = pl.ds(c * ko, ko)
        for i in list(range(1, cols)) + [0]:
            d = lax.rem(my_col + i, cols)
            high = [expand(yh_ref[d, l]) for l in range(kyl)]
            low = [expand(yl_ref[d, l]) for l in range(kyl)]
            acc = dot(lhs_ref[...], jnp.concatenate(high + high + low, 0))
            if i == 0:
                for v in range(2):
                    out_ref[pl.ds(my_col, 1), v, at, :] = acc[:, v * cells:(v + 1) * cells][None]
            else:
                for v in range(2):
                    csend[c, i - 1, v] = acc[:, v * cells:(v + 1) * cells]
                copy = pltpu.make_async_remote_copy(
                    csend.at[c, i - 1], out_ref.at[my_col, :, at, :], c_ss.at[c, i - 1], c_rs.at[c, i - 1],
                    device_id={"col": d}, device_id_type=MESH,
                )
                copy.start()
                c_copies.append(copy)
    for copy in c_copies:
        copy.wait_recv()
    for copy in z_copies + y_copies + [copy for started in x_copies for copy in started] + c_copies:
        copy.wait_send()


def z_back_kernel(channels, block, d_ref, vel_ref, tend_ref, step_ref, comb_ref, off_ref, tz_ref, out_ref, adv_ref):
    first = pl.program_id(0)
    depth = d_ref.shape[0] // channels

    @pl.when(first == 0)
    def _():
        adv_ref[...] = vel_ref[...] + step_ref[0] * tend_ref[...]

    for i in range(block):
        o = first * block + i
        high, low = split(d_ref[pl.ds(o, depth, stride=channels), :])
        lhs = jnp.concatenate([high, low, high], 0)
        spectral = lax.dot_general(lhs, tz_ref[...], (((0,), (0,)), ((), ())), preferred_element_type=F32)
        x = spectral + off_ref[o]
        for j in range(adv_ref.shape[0]):
            x = x + comb_ref[o, j] * adv_ref[j]
        inner = x * (0.7978845608028654 + 0.035677408136300125 * (x * x))
        half = 0.5 * x
        out_ref[i] = (half + half * jnp.tanh(inner)).astype(BF16)


def per_device(
    velocity, tendency, step_size, lift_weight, lift_bias, spectral_weight, local_weight, local_bias
):
    samples, width_in, a, b, nz = velocity.shape
    channels = lift_weight.shape[0]
    rows, cols = lax.axis_size("row"), lax.axis_size("col")
    full_x, full_y = a * rows, b * cols
    kzl, kyl = KZ // cols, KY // rows
    modes = kyl * kzl * KX
    cells = a * b
    vmem = pl.BlockSpec(memory_space=pltpu.VMEM)
    smem = pl.BlockSpec(memory_space=pltpu.SMEM)
    big = pltpu.CompilerParams(vmem_limit_bytes=48 * 1024 * 1024)

    lift4 = jnp.concatenate([lift_weight, lift_bias[:, None]], 1)
    group = width_in + 1
    eye = jnp.eye(channels, dtype=F32)
    lift_lanes = jnp.repeat(lift4, channels, axis=1)
    lift_full = jnp.tile(lift_lanes, (channels, 1))
    own = jnp.tile(jnp.repeat(eye, channels, axis=0), (1, group))
    masked = lift_full * own
    high = lax.reduce_precision(masked, 8, 7)
    lh, ll = high.astype(BF16), (masked - high).astype(BF16)
    lift_map = jnp.concatenate([lh, ll], 1)
    stored = spectral_weight.reshape(2 * modes, channels * channels)

    zc, zs = trig(np.arange(KZ), nz)
    rk = 2 * max(kzl, 4)
    zf = np.zeros((cols, 2, rk // 2, nz), np.float32)
    zf[:, :, :kzl] = np.stack([zc, -zs], 0).reshape(2, cols, kzl, nz).transpose(1, 0, 2, 3)
    zf = zf.reshape(cols * rk, nz)
    yc, ys = trig(waves(KY), full_y)
    xc, xs = trig(waves(KX), full_x)
    xf = np.concatenate([xc, xs], 0).astype(np.float32)
    selc = np.zeros((128, kzl, 2, group, channels), np.float32)
    sels = np.zeros_like(selc)
    for j in range(width_in):
        for k in range(kzl):
            re, im = j * rk + k, j * rk + rk // 2 + k
            selc[re, k, 0, j] = 1
            selc[im, k, 1, j] = 1
            sels[im, k, 0, j] = 1
            sels[re, k, 1, j] = -1
    selc = selc.reshape(128, -1)
    sels = sels.reshape(128, -1)
    xb = np.stack([np.stack([xc, -xs], 0), np.stack([xs, xc], 0)], 0)
    xb = xb.reshape(2, 2, KX, rows, a).transpose(3, 0, 4, 1, 2).reshape(rows * 2 * a, 2 * KX)
    xbh, xbl = np_halves(xb)
    xb3 = np.concatenate([xbh, xbh, xbl], 1)
    yb = np.stack([np.stack([yc, ys], 0), np.stack([-ys, yc], 0)], 0)
    yb = yb.reshape(2, 2, rows, kyl, cols, b).transpose(4, 3, 2, 0, 1, 5)
    yb = np.broadcast_to(yb[..., None, :], (cols, kyl, rows, 2, 2, a, b)).reshape(cols, kyl, rows * 2, 2 * cells)
    ybh, ybl = np_halves(yb)
    twice = np.where(np.arange(KZ) == 0, 1.0, 2.0)[:, None]
    zb = np.stack([twice * zc, -twice * zs], 0).reshape(2, cols, kzl, nz).transpose(1, 0, 2, 3).reshape(2 * KZ, nz)
    zbh, zbl = np_halves(zb)
    zb3 = np.concatenate([zbh, zbh, zbl], 0)
    yf = np.stack([yc, ys], 0).reshape(2, rows, kyl, 1, cols, 1, b)
    yf = (yf * np.eye(a).reshape(1, 1, 1, a, 1, a, 1)).reshape(2 * rows * kyl * a, cols * cells).T
    yfh, yfl = np_halves(yf)

    combined = jnp.dot(local_weight, lift_weight, precision=HIGHEST)
    offset = jnp.dot(local_weight, lift_bias, precision=HIGHEST) + local_bias
    origin = (lax.axis_index("row") == 0) & (lax.axis_index("col") == 0)
    last = np.arange(group * channels)[None, :] >= width_in * channels
    flag = jnp.where(jnp.asarray(last) & origin, 1.0, 0.0).astype(F32)

    results = []
    for sample in range(samples):
        vel = velocity[sample].reshape(width_in, cells, nz)
        tend = tendency[sample].reshape(width_in, cells, nz)
        step = step_size[sample].reshape(1)
        part = min(kzl, 4)
        chunks = kzl // part
        chunk_lanes = kyl * part * channels
        dma = lambda *shape: pltpu.SemaphoreType.DMA(shape)
        pencils_z = pl.pallas_call(
            functools.partial(layer_kernel, kyl, kzl, part, 1.0 / (full_x * full_y * nz)),
            out_shape=jax.ShapeDtypeStruct((cols, 2, kzl * channels, cells), F32),
            in_specs=[vmem, vmem, smem, vmem, vmem, vmem, pl.BlockSpec(memory_space=pl.ANY)] + [vmem] * 8,
            out_specs=vmem,
            scratch_shapes=[
                pltpu.VMEM(stored.shape, BF16),
                pltpu.VMEM((2 * modes, group * channels), F32),
                pltpu.VMEM((cols, width_in * rk, cells), F32),
                pltpu.VMEM((cols, width_in * rk, cells), F32),
                pltpu.VMEM((128, rows * kyl * a), F32),
                pltpu.VMEM((rows, kyl * a, 128), F32),
                pltpu.VMEM((rows, kyl * a, 128), F32),
                pltpu.VMEM((6 * KX, chunk_lanes), BF16),
                pltpu.VMEM((chunks, rows, 2 * a, chunk_lanes), F32),
                pltpu.VMEM((chunks, rows, 2 * a, chunk_lanes), F32),
                pltpu.VMEM((part * channels, 3 * kyl * rows * 2 * a), BF16),
                pltpu.VMEM((chunks, cols - 1, 2, part * channels, cells), F32),
                pltpu.SemaphoreType.DMA,
                dma(cols - 1), dma(cols - 1), dma(rows - 1), dma(rows - 1),
                dma(chunks, rows - 1), dma(chunks, rows - 1), dma(chunks, cols - 1), dma(chunks, cols - 1),
            ],
            compiler_params=pltpu.CompilerParams(
                vmem_limit_bytes=48 * 1024 * 1024, collective_id=0, has_side_effects=True
            ),
        )(
            vel, tend, step, jnp.asarray(zf), jnp.asarray(yfh), jnp.asarray(yfl), stored, lift_map, jnp.asarray(xf),
            jnp.asarray(selc, BF16), jnp.asarray(sels, BF16), flag, jnp.asarray(xb3), jnp.asarray(ybh), jnp.asarray(ybl),
        )
        pencils_z = pencils_z.reshape(cols * 2 * kzl * channels, cells)
        block = 4
        whole = lambda *shape: pl.BlockSpec(shape, lambda i: (0,) * len(shape))
        features = pl.pallas_call(
            functools.partial(z_back_kernel, channels, block),
            grid=(channels // block,),
            out_shape=jax.ShapeDtypeStruct((channels, cells, nz), BF16),
            in_specs=[
                whole(*pencils_z.shape), whole(width_in, cells, nz), whole(width_in, cells, nz),
                smem, smem, smem, whole(*zb3.shape),
            ],
            out_specs=pl.BlockSpec((block, cells, nz), lambda i: (i, 0, 0)),
            scratch_shapes=[pltpu.VMEM((width_in, cells, nz), F32)],
            compiler_params=big,
        )(
            pencils_z, vel, tend, step, combined, offset, jnp.asarray(zb3),
        )
        results.append(features.reshape(channels, a, b, nz))
    return jnp.stack(results, 0)


def solution(mesh):
    in_specs = (
        P(None, None, "row", "col", None),
        P(None, None, "row", "col", None),
        P(),
        P(),
        P(),
        P(None, "row", "col", None, None),
        P(),
        P(),
    )
    out_specs = P(None, None, "row", "col", None)
    return jax.shard_map(
        per_device, mesh=mesh, in_specs=in_specs, out_specs=out_specs, check_vma=False
    )
```

profile of v0, /device:TPU:9, one launch (start us, length us, event | category | flops | bytes accessed | tf_op | source)
XLA Modules:
  0.0 54.4 jit_solution(12546370816345428463)
XLA Ops:
  0.0 0.0 copy-start.10
  0.0 0.0 copy-start.3
  0.0 0.0 copy-start.4
  0.1 0.0 copy-start.12
  0.1 0.0 copy-start.5
  0.1 0.0 copy-start.6
  0.1 0.0 copy-start.11
  0.1 0.0 copy-start.2
  0.9 0.8 %and_select_fusion.flag_ref = f32[1,128]{1,0:T(1,128)S(1)} fusion(pred[1,128]{1,0:T(4,128)(4,1)} %constant.37.clone, pred[]{:T(512)S(6)} %and.11), kind=kLoop, calls=%fused_computation.10 | loop fusion | flops 256 | bytes 641 | tf_op jit(solution)/shard_map/jit(_where)/select_n | solution.py:312
  1.7 0.8 %fusion.off_ref = f32[32]{0:T(128)S(1)} fusion(f32[32]{0:T(128)} %param.26, f32[32,32]{1,0:T(8,128)S(1)} %copy-done, f32[32]{0:T(128)} %param.23), kind=kOutput, calls=%fused_computation.1 | convolution fusion | flops 12320 | bytes 4480 | tf_op jit(solution)/shard_map/dot_general | solution.py:309
  2.5 0.7 %pad_maximum_fusion.1 = f32[32,4]{0,1:T(4,128)S(1)} fusion(f32[32,1]{0,1:T(1,128)} %bitcast.32, f32[32,3]{0,1:T(4,128)} %param.22), kind=kLoop, calls=%fused_computation.9 | loop fusion | flops 128 | bytes 1024 | tf_op jit(solution)/shard_map/concatenate | solution.py:261
  3.3 0.1 copy.22
  3.4 0.8 %fusion.4.comb_ref = f32[32,3]{1,0:T(8,128)S(1)} fusion(f32[32,32]{1,0:T(8,128)S(1)} %copy-done, f32[32,3]{0,1:T(4,128)} %param.22), kind=kOutput, calls=%fused_computation.12 | convolution fusion | flops 36864 | bytes 4864 | tf_op jit(solution)/shard_map/dot_general | solution.py:308
  4.2 0.1 broadcast_in_dim.18
  4.3 0.1 tile.20
  4.4 1.0 %broadcast_in_dim.19 = f32[32,32,32]{1,0,2:T(8,128)} broadcast(f32[32,32]{0,1:T(8,128)S(1)} %fusion.2), dimensions={0,2} | broadcast | bytes 135168 | tf_op jit(solution)/shard_map/broadcast_in_dim | solution.py:266
  5.4 1.3 %tile.23 = f32[1024,32]{0,1:T(8,128)S(1)} reshape(f32[32,32,32]{1,0,2:T(8,128)} %broadcast_in_dim.19) | data formatting | bytes 262144 | tf_op jit(solution)/shard_map/tile | solution.py:266
  6.7 0.8 %tile.24 = f32[1024,4,32]{0,2,1:T(8,128)} broadcast(f32[1024,32]{0,1:T(8,128)S(1)} %tile.23), dimensions={0,2} | broadcast | bytes 655360 | tf_op jit(solution)/shard_map/tile | solution.py:266
  7.5 2.0 %copy.23 = f32[1024,128]{1,0:T(8,128)} copy(f32[1024,128]{0,1:T(8,128)} %bitcast.31) | data formatting | bytes 1048576 | tf_op jit(solution)/shard_map/tile | solution.py:266
  9.5 1.1 %reduce-precision_convert_fusion = (bf16[1024,128]{1,0:T(8,128)(2,1)S(1)}, bf16[1024,128]{1,0:T(8,128)(2,1)S(1)}) fusion(f32[1024,128]{1,0:T(8,128)} %copy.23, f32[32,128]{1,0:T(8,128)S(1)} %tile.20), kind=kLoop, calls=%fused_computation.3 | loop fusion | flops 655360 | bytes 1064960 | tf_op jit(solution)/shard_map/convert_element_type | solution.py:269
  10.7 0.1 pad_maximum_fusion.lift_ref
  10.9 0.0 copy-start.9
  10.9 37.3 %shard_map.181 = f32[4,2,256,128]{3,2,1,0:T(8,128)S(1)} custom-call(f32[3,128,256]{2,1,0:T(8,128)S(1)} %bitcast.26, f32[3,128,256]{2,1,0:T(8,128)S(1)} %bitcast.28, f32[1]{0:T(128)S(6)} %copy.26.step_ref, f32[64,256]{1,0:T(8,128)S(1)} %copy-done.11, bf16[512,512]{1,0:T(8,128)(2,1)S(1)} %copy-done.6, bf16[512,512]{1,0:T(8,128)(2,1)S(1)} %copy-done.5, ...), custom_call_target="tpu_custom_call" | custom-call | tf_op jit(solution)/shard_map/pallas_call | solution.py:323
  48.2 6.2 %shard_map.182 = bf16[32,128,256]{2,1,0:T(8,128)(2,1)} custom-call(f32[2048,128]{1,0:T(8,128)S(1)} %bitcast.25, f32[3,128,256]{2,1,0:T(8,128)S(1)} %bitcast.27, f32[3,128,256]{2,1,0:T(8,128)S(1)} %bitcast.29, f32[1]{0:T(128)S(6)} %copy.26.step_ref, f32[32,3]{1,0:T(8,128)S(1)} %fusion.4.comb_ref, f32[32]{0:T(128)S(1)} %fusion.off_ref, ...), custom_call_target="tpu_custom_call" | custom-call | tf_op jit(solution)/shard_map/pallas_call | solution.py:355
  (18 shorter events, 0.0 us)
Async XLA Ops:
  0.0 1.7 %copy-start = (f32[32,32]{1,0:T(8,128)S(1)}, f32[32,32]{1,0:T(8,128)}, u32[]{:S(2)}) copy-start(f32[32,32]{1,0:T(8,128)} %param.25) | copy-start | bytes 12292
  0.0 10.8 %copy-start.7 = (bf16[4,4,16,256]{3,2,1,0:T(8,128)(2,1)S(1)}, bf16[4,4,16,256]{3,2,1,0:T(8,128)(2,1)}, u32[]{:S(2)}) copy-start(bf16[4,4,16,256]{3,2,1,0:T(8,128)(2,1)} %constant.46.clone.yl_ref) | copy-start | bytes 393220
  0.0 10.8 %copy-start.8 = (bf16[4,4,16,256]{3,2,1,0:T(8,128)(2,1)S(1)}, bf16[4,4,16,256]{3,2,1,0:T(8,128)(2,1)}, u32[]{:S(2)}) copy-start(bf16[4,4,16,256]{3,2,1,0:T(8,128)(2,1)} %constant.45.clone.yh_ref) | copy-start | bytes 393220
  0.0 10.8 %copy-start.10 = (bf16[128,192]{1,0:T(8,128)(2,1)S(1)}, bf16[128,192]{1,0:T(8,128)(2,1)}, u32[]{:S(2)}) copy-start(bf16[128,192]{1,0:T(8,128)(2,1)} %constant.44.clone.xb_ref) | copy-start | bytes 147460
  0.0 10.8 %copy-start.3 = (bf16[128,2048]{1,0:T(8,128)(2,1)S(1)}, bf16[128,2048]{1,0:T(8,128)(2,1)}, u32[]{:S(2)}) copy-start(bf16[128,2048]{1,0:T(8,128)(2,1)} %constant.43.clone.sels_ref) | copy-start | bytes 1572868
  0.0 10.8 %copy-start.4 = (bf16[128,2048]{1,0:T(8,128)(2,1)S(1)}, bf16[128,2048]{1,0:T(8,128)(2,1)}, u32[]{:S(2)}) copy-start(bf16[128,2048]{1,0:T(8,128)(2,1)} %constant.42.clone.selc_ref) | copy-start | bytes 1572868
  0.1 10.8 %copy-start.12 = (f32[64,64]{1,0:T(8,128)S(1)}, f32[64,64]{1,0:T(8,128)}, u32[]{:S(2)}) copy-start(f32[64,64]{1,0:T(8,128)} %constant.41.clone.xf_ref) | copy-start | bytes 49156
  0.1 10.8 %copy-start.5 = (bf16[512,512]{1,0:T(8,128)(2,1)S(1)}, bf16[512,512]{1,0:T(8,128)(2,1)}, u32[]{:S(2)}) copy-start(bf16[512,512]{1,0:T(8,128)(2,1)} %constant.40.clone.yfl_ref) | copy-start | bytes 1572868
  0.1 10.7 %copy-start.6 = (bf16[512,512]{1,0:T(8,128)(2,1)S(1)}, bf16[512,512]{1,0:T(8,128)(2,1)}, u32[]{:S(2)}) copy-start(bf16[512,512]{1,0:T(8,128)(2,1)} %constant.39.clone.yfh_ref) | copy-start | bytes 1572868
  0.1 10.7 %copy-start.11 = (f32[64,256]{1,0:T(8,128)S(1)}, f32[64,256]{1,0:T(8,128)}, u32[]{:S(2)}) copy-start(f32[64,256]{1,0:T(8,128)} %constant.38.clone.zf_ref) | copy-start | bytes 196612
  0.1 10.7 %copy-start.2 = (f32[1,3,8,16,256]{4,3,2,1,0:T(8,128)S(1)}, f32[1,3,8,16,256]{4,3,2,1,0:T(8,128)}, u32[]{:S(2)}) copy-start(f32[1,3,8,16,256]{4,3,2,1,0:T(8,128)} %param.20) | copy-start | bytes 1179652
  0.1 10.7 %copy-start.1 = (f32[1,3,8,16,256]{4,3,2,1,0:T(8,128)S(1)}, f32[1,3,8,16,256]{4,3,2,1,0:T(8,128)}, u32[]{:S(2)}) copy-start(f32[1,3,8,16,256]{4,3,2,1,0:T(8,128)} %param.19) | copy-start | bytes 1179652
  10.9 37.3 %copy-start.9 = (bf16[192,256]{1,0:T(8,128)(2,1)S(1)}, bf16[192,256]{1,0:T(8,128)(2,1)}, u32[]{:S(2)}) copy-start(bf16[192,256]{1,0:T(8,128)(2,1)} %constant.47.clone.tz_ref) | copy-start | bytes 294916
where the time goes:
time: 54.7 us; the launch traced here: 54.4 us
  Pallas kernels  43.5 us (80%)
  local copies, waits for them, and re-layouts  5.5 us (10%)
  other arithmetic  2.74 us (5%)
  matrix products  1.61 us (3%)
  between operations  1.04 us (2%)
    pallas_call x1, Pallas kernels, per_device(): pl.pallas_call(functools.partial(layer_kernel, kyl, kzl, part, 1.0 / (ful...  37.3 us
    pallas_call x1, Pallas kernels, per_device(): pl.pallas_call(functools.partial(z_back_kernel, channels, block), grid=(c...  6.21 us
    another operation x3, local copies, waits for them, and re-layouts, per_device(): own = jnp.tile(jnp.repeat(eye, channels, axis=0), (1, group))  4.16 us
    convert_element_type x1, other arithmetic, per_device(): lh, ll = (high.astype(BF16), (masked - high).astype(BF16))  1.14 us

commit v1 on v0

v1 whole, which is shorter than its diff:
```python
import functools
import math

import jax
import jax.numpy as jnp
import numpy as np
from jax import lax
from jax.experimental import pallas as pl
from jax.experimental.pallas import tpu as pltpu
from jax.sharding import PartitionSpec as P

KX = 32
KY = 32
KZ = 32
LANES = 128
HIGHEST = lax.Precision.HIGHEST
F32 = jnp.float32
BF16 = jnp.bfloat16
MESH = pl.DeviceIdType.MESH


def waves(count):
    index = np.arange(count)
    return np.where(index < count // 2, index, index - count)


def trig(wave, length):
    angle = ((wave[:, None] * np.arange(length)[None, :]) % length) * (2.0 * math.pi / length)
    return np.cos(angle), np.sin(angle)


def np_halves(table):
    table = np.asarray(table, np.float32)
    high = table.astype(jnp.bfloat16)
    low = (table - high.astype(np.float32)).astype(jnp.bfloat16)
    return high, low


def split(x):
    high = x.astype(BF16)
    return high, (x - high.astype(F32)).astype(BF16)


def stacked(x):
    high = x.astype(BF16).astype(F32)
    return jnp.concatenate([high, x - high], 0).astype(BF16)


def dot(a, b):
    return jnp.dot(a, b, preferred_element_type=F32)


def dot_rows(a, b, precision=None):
    return lax.dot_general(a, b, (((0,), (0,)), ((), ())), precision=precision, preferred_element_type=F32)


def dot_lanes(a, b):
    return lax.dot_general(a, b, (((1,), (1,)), ((), ())), preferred_element_type=F32)


def iota(shape, axis):
    return lax.broadcasted_iota(jnp.int32, shape, axis)


def one_channel(d, row, adv_ref, tz):
    width_in = adv_ref.shape[0]
    d = d + jnp.where(iota(d.shape, 0) == 0, row(width_in), 0.0)
    high, low = split(d)
    x = dot_rows(jnp.concatenate([high, low, high], 0), tz)
    for j in range(width_in):
        weight = row(j)
        x = x + jnp.concatenate([weight] * (x.shape[1] // LANES), 1) * adv_ref[j]
    inner = x * (0.7978845608028654 + 0.035677408136300125 * (x * x))
    half = 0.5 * x
    return (half + half * jnp.tanh(inner)).astype(BF16)


def layer_kernel(
    kyl, kzl, oc, lag, vel_any, tend_any, step_any, lw_any, lb_any, cw_any, cb_any, zf_any, yfh_any, yfl_any, xf_any,
    sel_any, xb_any, yh_any, yl_any, tz_any, w_any, *rest,
):
    chunks = LANES // (oc * (lw_any.shape[0] + 1))
    if chunks > 1:
        feats_ref, rest = rest[0], rest[1:]
    else:
        feats_ref = None
    (
        dlast_ref, adv_ref, comb_ref, vel_ref, tend_ref, step_ref, lw_ref, lb_ref, cw_ref, cb_ref, zf_ref, yfh_ref,
        yfl_ref, xf_ref, sel_ref, xb_ref, yh_ref, yl_ref, tz_ref, w_ref, lift_ref, wl_ref, wt_ref, yexp_ref, zsend, zrecv,
        ypad, ysend, yrecv, amp_ref, xsend, xrecv, csend, crecv, in_sems, z_ss, z_rs, y_ss, y_rs, x_ss, x_rs, c_ss, c_rs,
    ) = rest
    rows, cols = lax.axis_size("row"), lax.axis_size("col")
    my_row, my_col = lax.axis_index("row"), lax.axis_index("col")
    width_in, cells, _ = vel_ref.shape
    channels = cw_ref.shape[0]
    group = width_in + 1
    freq = zf_ref.shape[0] // 2
    rk = freq // cols
    slots = kyl * kzl
    modes = slots * KX
    ko = kzl * oc

    loads = {}
    order = [
        ("vel", vel_any, vel_ref), ("tend", tend_any, tend_ref), ("step", step_any, step_ref), ("zf", zf_any, zf_ref),
        ("lw", lw_any, lw_ref), ("lb", lb_any, lb_ref), ("cw", cw_any, cw_ref), ("cb", cb_any, cb_ref),
        ("w", w_any, w_ref), ("yfh", yfh_any, yfh_ref), ("yfl", yfl_any, yfl_ref), ("yh", yh_any, yh_ref),
        ("yl", yl_any, yl_ref), ("xf", xf_any, xf_ref), ("sel", sel_any, sel_ref), ("xb", xb_any, xb_ref),
        ("tz", tz_any, tz_ref),
    ]
    for n, (name, source, target) in enumerate(order):
        loads[name] = pltpu.make_async_copy(source, target, in_sems.at[n])
        loads[name].start()

    def loaded(*names):
        for name in names:
            loads[name].wait()

    barrier = pltpu.get_barrier_semaphore()
    row_peers = [lax.rem(my_row + i, rows) for i in range(1, rows)]
    col_peers = [lax.rem(my_col + i, cols) for i in range(1, cols)]
    for peer in row_peers:
        pl.semaphore_signal(barrier, inc=1, device_id={"row": peer}, device_id_type=MESH)
    for peer in col_peers:
        pl.semaphore_signal(barrier, inc=1, device_id={"col": peer}, device_id_type=MESH)

    def send(source, target, sends, receives, **where):
        copy = pltpu.make_async_remote_copy(source, target, sends, receives, device_id=where, device_id_type=MESH)
        copy.start()
        return copy

    loaded("vel", "tend", "step", "zf")
    step = step_ref[0:1, 0:1]
    for j in range(width_in):
        adv = vel_ref[j] + step * tend_ref[j]
        adv_ref[j] = adv
        high, low = split(adv)
        both = dot_lanes(zf_ref[...], high)
        z = both[:freq] + both[freq:] + dot_lanes(zf_ref[0:freq, :], low)
        zsend[:, j * rk:(j + 1) * rk, :] = z.reshape(cols, rk, cells)
    pl.semaphore_wait(barrier, rows + cols - 2)
    z_copies = [
        send(zsend.at[peer], zrecv.at[my_col], z_ss.at[i], z_rs.at[i], col=peer) for i, peer in enumerate(col_peers)
    ]
    zrecv[pl.ds(my_col, 1)] = zsend[pl.ds(my_col, 1)]

    loaded("lw", "lb", "cw", "cb")
    eight = iota((8, channels), 0)
    lift = jnp.where(eight == width_in, lb_ref[...], 0.0)
    for j in range(width_in):
        lift = jnp.where(eight == j, lw_ref[j:j + 1, :], lift)
    block = iota((8, LANES), 1) // oc
    pick = jnp.where(block % group == iota((8, LANES), 0), 1.0, 0.0)
    spread = dot_rows(lift, pick, HIGHEST)
    high = spread.astype(BF16).astype(F32)
    low = spread - high
    lane = iota((channels, LANES), 1)
    owner = (lane // (oc * group)) * oc + lane % oc
    for o in range(channels):
        at = slice(o * channels, (o + 1) * channels)
        lift_ref[at, :LANES] = jnp.where(owner == o, high, 0.0).astype(BF16)
        lift_ref[at, LANES:] = jnp.where(owner == o, low, 0.0).astype(BF16)
    wide = (8, group * LANES)
    spread = dot_rows(lift, jnp.where(iota(wide, 1) // LANES == iota(wide, 0), 1.0, 0.0), HIGHEST)
    comb = jnp.dot(cw_ref[...], spread, precision=HIGHEST, preferred_element_type=F32)
    bias = jnp.where(eight == 0, cb_ref[...], 0.0)
    bias = dot_rows(bias, jnp.where(iota((8, LANES), 0) == 0, 1.0, 0.0), HIGHEST)
    comb_ref[:, :width_in * LANES] = comb[:, :width_in * LANES]
    comb_ref[:, width_in * LANES:] = comb[:, width_in * LANES:] + bias

    loaded("w")
    step_rows = modes // 2

    def weigh(n):
        at = slice(n * step_rows, (n + 1) * step_rows)
        both = dot(w_ref[at, :], lift_ref[...])
        wl_ref[at, :] = both[:, :LANES] + both[:, LANES:]

    weigh(0)
    weigh(1)
    loaded("yfh", "yfl")
    for copy in z_copies:
        copy.wait_recv()

    x = jnp.concatenate([zrecv[s] for s in range(cols)], 1)
    depth = width_in * rk
    halves = stacked(x)
    both = dot(halves, yfh_ref[...])
    y = both[:depth] + both[depth:] + dot(x.astype(BF16), yfl_ref[...])
    lanes = yfh_ref.shape[1] // 2
    wide = ypad.shape[1]
    parts = lanes // wide
    slot = ypad.shape[0] // parts
    ypad[...] = jnp.zeros_like(ypad)
    low_rows = iota((rk, lanes), 0) < rk // 2
    for j in range(width_in):
        here = y[j * rk:(j + 1) * rk]
        turned = pltpu.roll(here[:, lanes:], rk // 2, 0)
        here = here[:, :lanes] + jnp.where(low_rows, turned, -turned)
        for p in range(parts):
            ypad[p * slot + j * rk:p * slot + (j + 1) * rk, :] = here[:, p * wide:(p + 1) * wide]
    ysend[...] = jnp.transpose(ypad[...]).reshape(ysend.shape)
    y_copies = [
        send(ysend.at[peer], yrecv.at[my_row], y_ss.at[i], y_rs.at[i], row=peer) for i, peer in enumerate(row_peers)
    ]
    yrecv[pl.ds(my_row, 1)] = ysend[pl.ds(my_row, 1)]

    weigh(2)
    weigh(3)

    def turn(n, carry):
        ri, at = n // (KX // 8), (n % (KX // 8)) * 8
        held = [wl_ref[pl.ds(pl.multiple_of(ri * modes + s * KX + at, 8), 8), :] for s in range(slots)]
        place = iota((8, LANES), 1) // oc
        bit = 1
        while bit < slots:
            upper = (place // bit) % 2 == 1
            for s in range(slots):
                if not s & bit:
                    a, b = held[s], held[s | bit]
                    held[s] = jnp.where(upper, pltpu.roll(b, bit * oc, 1), a)
                    held[s | bit] = jnp.where(upper, b, pltpu.roll(a, LANES - bit * oc, 1))
            bit *= 2
        for s in range(slots):
            wt_ref[ri, s, pl.ds(pl.multiple_of(at, 8), 8), :] = held[s]
        return carry

    lax.fori_loop(0, 2 * (KX // 8), turn, 0)

    loaded("yh", "yl")
    pairs = 2 * rows
    a = xsend.shape[2] // 2
    total = pairs * a
    width = 2 * cells
    same = iota((pairs, a, width), 1) == (iota((pairs, a, width), 2) // (cells // a)) % a

    def expand(d, carry):
        for h, table in enumerate((yh_ref, yl_ref)):
            for l in range(kyl):
                full = jnp.where(same, table[d, l].astype(F32)[:, None, :], 0.0)
                yexp_ref[d, h, l * total:(l + 1) * total, :] = full.reshape(total, width).astype(BF16)
        return carry

    lax.fori_loop(0, cols, expand, 0)
    loaded("xf", "sel", "xb", "tz")
    for copy in y_copies:
        copy.wait_recv()

    deep = yrecv.shape[1] // a
    is_re = (iota((rows * a, LANES), 1) % rk) < rk // 2
    plain, cross = [], []
    for l in range(deep):
        u = yrecv[:, l * a:(l + 1) * a, :].reshape(rows * a, LANES)
        plain.append(u)
        cross.append(jnp.where(is_re, pltpu.roll(u, LANES - rk // 2, 1), -pltpu.roll(u, rk // 2, 1)))
    u = jnp.concatenate([jnp.concatenate(plain, 1), jnp.concatenate(cross, 1)], 0)
    high, low = split(u)
    both = dot(xf_ref[...], high)
    q = both[:KX] + both[KX:] + dot(xf_ref[0:KX, :], low)
    both = dot(stacked(q), sel_ref[...])
    amp_ref[...] = both[:KX] + both[KX:]
    origin = jnp.where((my_row == 0) & (my_col == 0), 1.0, 0.0)
    flag = jnp.where((iota((KX, LANES), 0) == 0) & (iota((KX, LANES), 1) < oc), origin, 0.0)

    x_copies = []
    for c in range(chunks):
        pr = wt_ref[0, c * group + width_in] * flag
        pi = wt_ref[1, c * group + width_in] * flag
        for j in range(width_in):
            wr, wi = wt_ref[0, c * group + j], wt_ref[1, c * group + j]
            ar = amp_ref[:, (2 * j) * LANES:(2 * j + 1) * LANES]
            ai = amp_ref[:, (2 * j + 1) * LANES:(2 * j + 2) * LANES]
            pr = pr + (wr * ar - wi * ai)
            pi = pi + (wr * ai + wi * ar)
        high, low = split(jnp.concatenate([pr, pi], 0))
        xsend[c] = dot(xb_ref[...], jnp.concatenate([high, low, high], 0)).reshape(xsend.shape[1:])
        x_copies.append([
            send(xsend.at[c, peer], xrecv.at[c, my_row], x_ss.at[c, i], x_rs.at[c, i], row=peer)
            for i, peer in enumerate(row_peers)
        ])
        xrecv[c, pl.ds(my_row, 1)] = xsend[c, pl.ds(my_row, 1)]

    tz = tz_ref[...]
    c_copies = []

    def landing(c):
        return dlast_ref if c == chunks - 1 else crecv.at[c]

    def inverse_y(c):
        for copy in x_copies[c]:
            copy.wait_recv()
        turned = jnp.transpose(xrecv[c].reshape(total, LANES))
        held = jnp.concatenate([turned[l * ko:(l + 1) * ko] for l in range(kyl)], 1)
        halves = stacked(held)
        at = pl.ds(pl.multiple_of(my_col * 2 * ko, 2 * ko), 2 * ko)
        started = []
        for i in list(range(1, cols)) + [0]:
            d = lax.rem(my_col + i, cols)
            both = dot(halves, yexp_ref[d, 0])
            acc = both[:ko] + both[ko:] + dot(halves[:ko], yexp_ref[d, 1])
            acc = jnp.concatenate([acc[:, v * cells:(v + 1) * cells] for v in range(2)], 0)
            if i == 0:
                landing(c)[at, :] = acc
            else:
                csend[c, i - 1] = acc
                started.append(
                    send(csend.at[c, i - 1], landing(c).at[at, :], c_ss.at[c, i - 1], c_rs.at[c, i - 1], col=d)
                )
        c_copies.append(started)

    def inverse_z(c):
        for copy in c_copies[c]:
            copy.wait_recv()
        for i in range(oc):
            o = c * oc + i
            row = lambda j: comb_ref[o:o + 1, j * LANES:(j + 1) * LANES]
            d = crecv[c, pl.ds(i, cols * 2 * kzl, stride=oc), :]
            feats_ref[o] = one_channel(d, row, adv_ref, tz)

    for c in range(chunks):
        inverse_y(c)
        if 0 <= c - lag < chunks - 1:
            inverse_z(c - lag)
    for c in range(max(chunks - lag, 0), chunks - 1):
        inverse_z(c)
    for copy in c_copies[chunks - 1]:
        copy.wait_recv()
    for copies in [z_copies, y_copies] + x_copies + c_copies:
        for copy in copies:
            copy.wait_send()


def finish_kernel(oc, depth, *refs):
    if len(refs) == 8:
        feats_ref, refs = refs[0], refs[1:]
        first = feats_ref.shape[0]
    else:
        feats_ref, first = None, 0
    d_ref, adv_ref, comb_ref, tz_ref, out_ref, last_ref, sems = refs
    copies = []
    if feats_ref is not None:
        copies.append(pltpu.make_async_copy(feats_ref, out_ref.at[pl.ds(0, first)], sems.at[oc]))
        copies[0].start()
    for i in range(oc):
        o = first + i
        row = lambda j: comb_ref[o:o + 1, j * LANES:(j + 1) * LANES]
        last_ref[i] = one_channel(d_ref[pl.ds(i, depth, stride=oc), :], row, adv_ref, tz_ref[...])
        copy = pltpu.make_async_copy(last_ref.at[pl.ds(i, 1)], out_ref.at[pl.ds(o, 1)], sems.at[i])
        copy.start()
        copies.append(copy)
    for copy in copies:
        copy.wait()


def per_device(
    velocity, tendency, step_size, lift_weight, lift_bias, spectral_weight, local_weight, local_bias
):
    samples, width_in, a, b, nz = velocity.shape
    channels = lift_weight.shape[0]
    rows, cols = lax.axis_size("row"), lax.axis_size("col")
    full_x, full_y = a * rows, b * cols
    kzl, kyl = KZ // cols, KY // rows
    slots = kyl * kzl
    modes = slots * KX
    cells = a * b
    group = width_in + 1
    oc = LANES // slots
    chunks = channels // oc
    ko = kzl * oc
    lag = 3
    vmem = pl.BlockSpec(memory_space=pltpu.VMEM)
    anywhere = pl.BlockSpec(memory_space=pl.ANY)
    stored = spectral_weight.reshape(2 * modes, channels * channels)

    zc, zs = trig(np.arange(KZ), nz)
    rk = 2 * max(kzl, 4)
    zf = np.zeros((cols, 2, rk // 2, nz), np.float32)
    zf[:, :, :kzl] = np.stack([zc, -zs], 0).reshape(2, cols, kzl, nz).transpose(1, 0, 2, 3)
    zf2 = np.concatenate(np_halves(zf.reshape(cols * rk, nz)), 0)
    yc, ys = trig(waves(KY), full_y)
    xc, xs = trig(waves(KX), full_x)
    scale = 1.0 / (full_x * full_y * nz)
    xf2 = np.concatenate(np_halves(np.concatenate([xc, xs], 1) * scale), 0)
    parts = 2
    deep = kyl // parts
    slot = LANES // parts
    yf = np.stack([yc, ys], 0).reshape(2, rows, deep, parts, 1, cols, 1, b)
    yf = yf * np.eye(a).reshape(1, 1, 1, 1, a, 1, a, 1)
    yf = yf.transpose(0, 3, 1, 2, 4, 5, 6, 7).reshape(2 * parts * rows * deep * a, cols * cells).T
    yfh, yfl = np_halves(yf)
    sel = np.zeros((deep, parts, slot, width_in, 2, kyl, kzl, oc), np.float32)
    for l in range(kyl):
        for j in range(width_in):
            for ri in range(2):
                for k in range(kzl):
                    sel[l // parts, l % parts, j * rk + ri * (rk // 2) + k, j, ri, l, k] = 1
    sel = sel.reshape(deep * LANES, width_in * 2 * LANES)
    xb = np.stack([np.stack([xc, -xs], 0), np.stack([xs, xc], 0)], 0)
    xb = xb.reshape(2, 2, KX, rows, a).transpose(3, 0, 4, 1, 2).reshape(rows * 2 * a, 2 * KX)
    xbh, xbl = np_halves(xb)
    xb3 = np.concatenate([xbh, xbh, xbl], 1)
    yb = np.stack([np.stack([yc, ys], 0), np.stack([-ys, yc], 0)], 0)
    yb = yb.reshape(2, 2, rows, kyl, cols, b).transpose(4, 3, 2, 0, 1, 5)
    yb = np.broadcast_to(yb[..., None, :], (cols, kyl, rows, 2, 2, a, b)).reshape(cols, kyl, rows * 2, 2 * cells)
    ybh, ybl = np_halves(yb)
    twice = np.where(np.arange(KZ) == 0, 1.0, 2.0)[:, None]
    zb = np.stack([twice * zc, -twice * zs], 0).reshape(2, cols, kzl, nz).transpose(1, 0, 2, 3).reshape(2 * KZ, nz)
    zbh, zbl = np_halves(zb)
    zb3 = np.concatenate([zbh, zbh, zbl], 0)
    tz = jnp.asarray(zb3)

    results = []
    for sample in range(samples):
        inputs = [
            velocity[sample].reshape(width_in, cells, nz), tendency[sample].reshape(width_in, cells, nz),
            step_size[sample].reshape(1, 1), lift_weight.T, lift_bias.reshape(1, channels), local_weight,
            local_bias.reshape(1, channels), jnp.asarray(zf2), jnp.asarray(yfh), jnp.asarray(yfl), jnp.asarray(xf2),
            jnp.asarray(sel, BF16), jnp.asarray(xb3), jnp.asarray(ybh), jnp.asarray(ybl), tz, stored,
        ]
        dma = lambda *shape: pltpu.SemaphoreType.DMA(shape)
        first = channels - oc
        outs = [
            jax.ShapeDtypeStruct((cols * 2 * ko, cells), F32),
            jax.ShapeDtypeStruct((width_in, cells, nz), F32),
            jax.ShapeDtypeStruct((channels, group * LANES), F32),
        ]
        if first:
            outs = [jax.ShapeDtypeStruct((first, cells, nz), BF16)] + outs
        held = pl.pallas_call(
            functools.partial(layer_kernel, kyl, kzl, oc, lag),
            out_shape=outs,
            in_specs=[anywhere] * len(inputs),
            out_specs=[vmem] * len(outs),
            scratch_shapes=[pltpu.VMEM(x.shape, x.dtype) for x in inputs] + [
                pltpu.VMEM((channels * channels, 2 * LANES), BF16),
                pltpu.VMEM((2 * modes, LANES), F32),
                pltpu.VMEM((2, slots, KX, LANES), F32),
                pltpu.VMEM((cols, 2, kyl * rows * 2 * a, 2 * cells), BF16),
                pltpu.VMEM((cols, width_in * rk, cells), F32),
                pltpu.VMEM((cols, width_in * rk, cells), F32),
                pltpu.VMEM((parts * slot, rows * deep * a), F32),
                pltpu.VMEM((rows, deep * a, LANES), F32),
                pltpu.VMEM((rows, deep * a, LANES), F32),
                pltpu.VMEM((KX, width_in * 2 * LANES), F32),
                pltpu.VMEM((chunks, rows, 2 * a, LANES), F32),
                pltpu.VMEM((chunks, rows, 2 * a, LANES), F32),
                pltpu.VMEM((chunks, cols - 1, 2 * ko, cells), F32),
                pltpu.VMEM((chunks, cols * 2 * ko, cells), F32),
                dma(len(inputs)),
                dma(cols - 1), dma(cols - 1), dma(rows - 1), dma(rows - 1),
                dma(chunks, rows - 1), dma(chunks, rows - 1), dma(chunks, cols - 1), dma(chunks, cols - 1),
            ],
            compiler_params=pltpu.CompilerParams(
                vmem_limit_bytes=40 * 1024 * 1024, collective_id=0, has_side_effects=True
            ),
        )(*inputs)
        features = pl.pallas_call(
            functools.partial(finish_kernel, oc, cols * 2 * kzl),
            out_shape=jax.ShapeDtypeStruct((channels, cells, nz), BF16),
            in_specs=[vmem] * (len(held) + 1),
            out_specs=anywhere,
            scratch_shapes=[pltpu.VMEM((oc, cells, nz), BF16), dma(oc + 1)],
            compiler_params=pltpu.CompilerParams(vmem_limit_bytes=16 * 1024 * 1024),
        )(*held, tz)
        results.append(features.reshape(channels, a, b, nz))
    return jnp.stack(results, 0)


def solution(mesh):
    in_specs = (
        P(None, None, "row", "col", None),
        P(None, None, "row", "col", None),
        P(),
        P(),
        P(),
        P(None, "row", "col", None, None),
        P(),
        P(),
    )
    out_specs = P(None, None, "row", "col", None)
    return jax.shard_map(
        per_device, mesh=mesh, in_specs=in_specs, out_specs=out_specs, check_vma=False
    )
```

time: 54.7 us -> 55.8 us (1.020)
  the two profiles are of different devices: /device:TPU:9 before, /device:TPU:0 now
where the time goes in v1:
time: 55.8 us; the launch traced here: 55.1 us
  Pallas kernels  39.4 us (71%)
  local copies, waits for them, and re-layouts  15.1 us (27%)
  between operations  0.68 us (1%)
    pallas_call x1, Pallas kernels, per_device(): pl.pallas_call(functools.partial(layer_kernel, kyl, kzl, oc, lag), out_sh...  38 us
    unnamed x32, local copies, waits for them, and re-layouts  15.1 us
    pallas_call x1, Pallas kernels, per_device(): pl.pallas_call(functools.partial(finish_kernel, oc, cols * 2 * kzl), out_...  1.35 us

profile of v1, /device:TPU:0, one launch (start us, length us, event | category | flops | bytes accessed | tf_op | source)
XLA Modules:
  0.0 55.1 jit_solution(8326842569536669073)
XLA Ops:
  0.7 0.0 copy-start
  0.7 2.2 %copy-done = bf16[2,4,8,32,1024]{4,3,2,1,0:T(8,128)(2,1)S(1)} copy-done((bf16[2,4,8,32,1024]{4,3,2,1,0:T(8,128)(2,1)S(1)}, bf16[2,4,8,32,1024]{4,3,2,1,0:T(8,128)(2,1)}, u32[]{:S(2)}) %copy-start) | copy-done | bytes 4194328
  2.8 1.0 %copy-done.1 = bf16[512,512]{1,0:T(8,128)(2,1)S(1)} copy-done((bf16[512,512]{1,0:T(8,128)(2,1)S(1)}, bf16[512,512]{1,0:T(8,128)(2,1)}, u32[]{:S(2)}) %copy-start.1) | copy-done | bytes 524312
  3.9 0.0 copy-start.2
  3.9 1.0 %copy-done.2 = bf16[512,512]{1,0:T(8,128)(2,1)S(1)} copy-done((bf16[512,512]{1,0:T(8,128)(2,1)S(1)}, bf16[512,512]{1,0:T(8,128)(2,1)}, u32[]{:S(2)}) %copy-start.2) | copy-done | bytes 524312
  4.9 0.0 copy-start.3
  4.9 1.0 %copy-done.3 = f32[1,3,8,16,256]{4,3,2,1,0:T(8,128)S(1)} copy-done((f32[1,3,8,16,256]{4,3,2,1,0:T(8,128)S(1)}, f32[1,3,8,16,256]{4,3,2,1,0:T(8,128)}, u32[]{:S(2)}) %copy-start.3) | copy-done | bytes 393240
  5.9 0.0 copy-start.4
  5.9 1.0 %copy-done.4 = f32[1,3,8,16,256]{4,3,2,1,0:T(8,128)S(1)} copy-done((f32[1,3,8,16,256]{4,3,2,1,0:T(8,128)S(1)}, f32[1,3,8,16,256]{4,3,2,1,0:T(8,128)}, u32[]{:S(2)}) %copy-start.4) | copy-done | bytes 393240
  6.9 0.0 copy-start.5
  6.9 1.0 %copy-done.5 = bf16[256,768]{1,0:T(8,128)(2,1)S(1)} copy-done((bf16[256,768]{1,0:T(8,128)(2,1)S(1)}, bf16[256,768]{1,0:T(8,128)(2,1)}, u32[]{:S(2)}) %copy-start.5) | copy-done | bytes 393240
  7.9 0.0 copy-start.6
  7.9 0.9 %copy-done.6 = bf16[192,256]{1,0:T(8,128)(2,1)S(1)} copy-done((bf16[192,256]{1,0:T(8,128)(2,1)S(1)}, bf16[192,256]{1,0:T(8,128)(2,1)}, u32[]{:S(2)}) %copy-start.6) | copy-done | bytes 98328
  8.8 0.9 %copy-done.7 = bf16[4,4,16,256]{3,2,1,0:T(8,128)(2,1)S(1)} copy-done((bf16[4,4,16,256]{3,2,1,0:T(8,128)(2,1)S(1)}, bf16[4,4,16,256]{3,2,1,0:T(8,128)(2,1)}, u32[]{:S(2)}) %copy-start.7) | copy-done | bytes 131096
  9.7 0.9 %copy-done.8 = bf16[4,4,16,256]{3,2,1,0:T(8,128)(2,1)S(1)} copy-done((bf16[4,4,16,256]{3,2,1,0:T(8,128)(2,1)S(1)}, bf16[4,4,16,256]{3,2,1,0:T(8,128)(2,1)}, u32[]{:S(2)}) %copy-start.8) | copy-done | bytes 131096
  10.6 0.8 %copy-done.9 = bf16[128,192]{1,0:T(8,128)(2,1)S(1)} copy-done((bf16[128,192]{1,0:T(8,128)(2,1)S(1)}, bf16[128,192]{1,0:T(8,128)(2,1)}, u32[]{:S(2)}) %copy-start.9) | copy-done | bytes 49176
  11.5 0.8 %copy-done.10 = bf16[128,256]{1,0:T(8,128)(2,1)S(1)} copy-done((bf16[128,256]{1,0:T(8,128)(2,1)S(1)}, bf16[128,256]{1,0:T(8,128)(2,1)}, u32[]{:S(2)}) %copy-start.10) | copy-done | bytes 65560
  12.3 0.7 %copy-done.11 = f32[32,32]{1,0:T(8,128)S(1)} copy-done((f32[32,32]{1,0:T(8,128)S(1)}, f32[32,32]{1,0:T(8,128)}, u32[]{:S(2)}) %copy-start.11) | copy-done | bytes 4120
  13.0 0.7 %copy-done.12 = bf16[64,128]{1,0:T(8,128)(2,1)S(1)} copy-done((bf16[64,128]{1,0:T(8,128)(2,1)S(1)}, bf16[64,128]{1,0:T(8,128)(2,1)}, u32[]{:S(2)}) %copy-start.12) | copy-done | bytes 16408
  13.7 0.7 %copy-done.13 = f32[32,3]{0,1:T(4,128)S(1)} copy-done((f32[32,3]{0,1:T(4,128)S(1)}, f32[32,3]{0,1:T(4,128)}, u32[]{:S(2)}) %copy-start.13) | copy-done | bytes 408
  14.4 0.7 %copy-done.14 = f32[32]{0:T(128)S(1)} copy-done((f32[32]{0:T(128)S(1)}, f32[32]{0:T(128)}, u32[]{:S(2)}) %copy-start.14) | copy-done | bytes 152
  15.1 0.7 %copy-done.15 = f32[32]{0:T(128)S(1)} copy-done((f32[32]{0:T(128)S(1)}, f32[32]{0:T(128)}, u32[]{:S(2)}) %copy-start.15) | copy-done | bytes 152
  15.7 38.0 %shard_map.163 = (bf16[28,128,256]{2,1,0:T(8,128)(2,1)S(1)}, f32[256,128]{1,0:T(8,128)S(1)}, f32[3,128,256]{2,1,0:T(8,128)S(1)}, f32[32,512]{1,0:T(8,128)S(1)}) custom-call(f32[3,128,256]{2,1,0:T(8,128)S(1)} %bitcast.10, f32[3,128,256]{2,1,0:T(8,128)S(1)} %bitcast.11, f32[1,1]{1,0:T(1,128)} %bitcast.8.step_any, f32[3,32]{1,0:T(4,128)S(1)} %bitcast.12, ...), custom_call_target="tpu_custom_call" | custom-call | tf_op jit(solution)/shard_map/pallas_call | solution.py:429
  53.8 1.3 %shard_map.164 = bf16[32,128,256]{2,1,0:T(8,128)(2,1)} custom-call(bf16[28,128,256]{2,1,0:T(8,128)(2,1)S(1)} %get-tuple-element.9.refs_0_, f32[256,128]{1,0:T(8,128)S(1)} %get-tuple-element.10.refs_1_, f32[3,128,256]{2,1,0:T(8,128)S(1)} %get-tuple-element.11.refs_2_, f32[32,512]{1,0:T(8,128)S(1)} %get-tuple-element.12.refs_3_, bf16[192,256]{1,0:T(8,128)(2,1)S(1)} %copy-done.6), custom_call_target="tpu_custom_call" | custom-call | tf_op jit(solution)/shard_map/pallas_call | solution.py:457
  (10 shorter events, 0.0 us)
Async XLA Ops:
  0.7 2.2 %copy-start = (bf16[2,4,8,32,1024]{4,3,2,1,0:T(8,128)(2,1)S(1)}, bf16[2,4,8,32,1024]{4,3,2,1,0:T(8,128)(2,1)}, u32[]{:S(2)}) copy-start(bf16[2,4,8,32,1024]{4,3,2,1,0:T(8,128)(2,1)} %param.22) | copy-start | bytes 12582916
  2.8 1.0 %copy-start.1 = (bf16[512,512]{1,0:T(8,128)(2,1)S(1)}, bf16[512,512]{1,0:T(8,128)(2,1)}, u32[]{:S(2)}) copy-start(bf16[512,512]{1,0:T(8,128)(2,1)} %constant.21.clone.yfl_any) | copy-start | bytes 1572868
  3.9 1.0 %copy-start.2 = (bf16[512,512]{1,0:T(8,128)(2,1)S(1)}, bf16[512,512]{1,0:T(8,128)(2,1)}, u32[]{:S(2)}) copy-start(bf16[512,512]{1,0:T(8,128)(2,1)} %constant.20.clone.yfh_any) | copy-start | bytes 1572868
  4.9 1.0 %copy-start.3 = (f32[1,3,8,16,256]{4,3,2,1,0:T(8,128)S(1)}, f32[1,3,8,16,256]{4,3,2,1,0:T(8,128)}, u32[]{:S(2)}) copy-start(f32[1,3,8,16,256]{4,3,2,1,0:T(8,128)} %param.17) | copy-start | bytes 1179652
  5.9 1.0 %copy-start.4 = (f32[1,3,8,16,256]{4,3,2,1,0:T(8,128)S(1)}, f32[1,3,8,16,256]{4,3,2,1,0:T(8,128)}, u32[]{:S(2)}) copy-start(f32[1,3,8,16,256]{4,3,2,1,0:T(8,128)} %param.18) | copy-start | bytes 1179652
  6.9 1.0 %copy-start.5 = (bf16[256,768]{1,0:T(8,128)(2,1)S(1)}, bf16[256,768]{1,0:T(8,128)(2,1)}, u32[]{:S(2)}) copy-start(bf16[256,768]{1,0:T(8,128)(2,1)} %constant.23.clone.sel_any) | copy-start | bytes 1179652
  7.9 0.9 %copy-start.6 = (bf16[192,256]{1,0:T(8,128)(2,1)S(1)}, bf16[192,256]{1,0:T(8,128)(2,1)}, u32[]{:S(2)}) copy-start(bf16[192,256]{1,0:T(8,128)(2,1)} %constant.18.clone.tz_any.refs_4_) | copy-start | bytes 294916
  8.8 0.9 %copy-start.7 = (bf16[4,4,16,256]{3,2,1,0:T(8,128)(2,1)S(1)}, bf16[4,4,16,256]{3,2,1,0:T(8,128)(2,1)}, u32[]{:S(2)}) copy-start(bf16[4,4,16,256]{3,2,1,0:T(8,128)(2,1)} %constant.26.clone.yl_any) | copy-start | bytes 393220
  9.7 0.9 %copy-start.8 = (bf16[4,4,16,256]{3,2,1,0:T(8,128)(2,1)S(1)}, bf16[4,4,16,256]{3,2,1,0:T(8,128)(2,1)}, u32[]{:S(2)}) copy-start(bf16[4,4,16,256]{3,2,1,0:T(8,128)(2,1)} %constant.25.clone.yh_any) | copy-start | bytes 393220
  10.6 0.8 %copy-start.9 = (bf16[128,192]{1,0:T(8,128)(2,1)S(1)}, bf16[128,192]{1,0:T(8,128)(2,1)}, u32[]{:S(2)}) copy-start(bf16[128,192]{1,0:T(8,128)(2,1)} %constant.24.clone.xb_any) | copy-start | bytes 147460
  11.5 0.8 %copy-start.10 = (bf16[128,256]{1,0:T(8,128)(2,1)S(1)}, bf16[128,256]{1,0:T(8,128)(2,1)}, u32[]{:S(2)}) copy-start(bf16[128,256]{1,0:T(8,128)(2,1)} %constant.19.clone.zf_any) | copy-start | bytes 196612
  12.3 0.7 %copy-start.11 = (f32[32,32]{1,0:T(8,128)S(1)}, f32[32,32]{1,0:T(8,128)}, u32[]{:S(2)}) copy-start(f32[32,32]{1,0:T(8,128)} %cw_any.1) | copy-start | bytes 12292
  13.0 0.7 %copy-start.12 = (bf16[64,128]{1,0:T(8,128)(2,1)S(1)}, bf16[64,128]{1,0:T(8,128)(2,1)}, u32[]{:S(2)}) copy-start(bf16[64,128]{1,0:T(8,128)(2,1)} %constant.22.clone.xf_any) | copy-start | bytes 49156
  13.7 0.7 %copy-start.13 = (f32[32,3]{0,1:T(4,128)S(1)}, f32[32,3]{0,1:T(4,128)}, u32[]{:S(2)}) copy-start(f32[32,3]{0,1:T(4,128)} %param.20) | copy-start | bytes 1156
  14.4 0.7 %copy-start.14 = (f32[32]{0:T(128)S(1)}, f32[32]{0:T(128)}, u32[]{:S(2)}) copy-start(f32[32]{0:T(128)} %param.21) | copy-start | bytes 388
  15.1 0.7 %copy-start.15 = (f32[32]{0:T(128)S(1)}, f32[32]{0:T(128)}, u32[]{:S(2)}) copy-start(f32[32]{0:T(128)} %param.24) | copy-start | bytes 388

commit v2 on v1

--- a/solution.py
+++ b/solution.py
@@ -453,7 +453,7 @@
             compiler_params=pltpu.CompilerParams(
                 vmem_limit_bytes=40 * 1024 * 1024, collective_id=0, has_side_effects=True
             ),
-        )(*inputs)
+        )(*[x if x.size == 1 else pltpu.with_memory_space_constraint(x, pltpu.HBM) for x in inputs])
         features = pl.pallas_call(
             functools.partial(finish_kernel, oc, cols * 2 * kzl),
             out_shape=jax.ShapeDtypeStruct((channels, cells, nz), BF16),

time: 55.8 us -> 38.6 us (0.69)
  local copies, waits for them, and re-layouts: 15.1 us -> 0.01 us
  Pallas kernels: 39.4 us -> 37.8 us
    unnamed x32 -> x2, local copies, waits for them, and re-layouts: 15.1 us -> 0.01 us
    pallas_call x1, Pallas kernels: 38 us -> 36.4 us  [per_device(): pl.pallas_call(functools.partial(layer_kernel, kyl, kzl, oc, lag), out_sh...]
where the time goes in v2:
time: 38.6 us; the launch traced here: 38.4 us
  Pallas kernels  37.8 us (98%)
  between operations  0.68 us (2%)
    pallas_call x1, Pallas kernels, per_device(): pl.pallas_call(functools.partial(layer_kernel, kyl, kzl, oc, lag), out_sh...  36.4 us
    pallas_call x1, Pallas kernels, per_device(): pl.pallas_call(functools.partial(finish_kernel, oc, cols * 2 * kzl), out_...  1.35 us

profile of v2, /device:TPU:0, one launch (start us, length us, event | category | flops | bytes accessed | tf_op | source)
XLA Modules:
  0.0 38.4 jit_solution(7568746848185340182)
XLA Ops:
  0.7 0.0 copy-start
  0.7 36.4 %shard_map.163 = (bf16[28,128,256]{2,1,0:T(8,128)(2,1)S(1)}, f32[256,128]{1,0:T(8,128)S(1)}, f32[3,128,256]{2,1,0:T(8,128)S(1)}, f32[32,512]{1,0:T(8,128)S(1)}) custom-call(f32[3,128,256]{2,1,0:T(8,128)} %bitcast.10, f32[3,128,256]{2,1,0:T(8,128)} %bitcast.11, f32[1,1]{1,0:T(1,128)} %bitcast.8.step_any, f32[3,32]{1,0:T(4,128)} %bitcast.12, ...), custom_call_target="tpu_custom_call" | custom-call | tf_op jit(solution)/shard_map/pallas_call | solution.py:429
  37.1 0.0 copy-done
  37.1 1.3 %shard_map.164 = bf16[32,128,256]{2,1,0:T(8,128)(2,1)} custom-call(bf16[28,128,256]{2,1,0:T(8,128)(2,1)S(1)} %get-tuple-element.9.refs_0_, f32[256,128]{1,0:T(8,128)S(1)} %get-tuple-element.10.refs_1_, f32[3,128,256]{2,1,0:T(8,128)S(1)} %get-tuple-element.11.refs_2_, f32[32,512]{1,0:T(8,128)S(1)} %get-tuple-element.12.refs_3_, bf16[192,256]{1,0:T(8,128)(2,1)S(1)} %copy-done), custom_call_target="tpu_custom_call" | custom-call | tf_op jit(solution)/shard_map/pallas_call | solution.py:457
Async XLA Ops:
  0.7 36.4 %copy-start = (bf16[192,256]{1,0:T(8,128)(2,1)S(1)}, bf16[192,256]{1,0:T(8,128)(2,1)}, u32[]{:S(2)}) copy-start(bf16[192,256]{1,0:T(8,128)(2,1)} %constant.18.clone.tz_any.refs_4_) | copy-start | bytes 294916

commit v3 on v2

--- a/solution.py
+++ b/solution.py
@@ -76,8 +76,8 @@
 
 
 def layer_kernel(
-    kyl, kzl, oc, lag, vel_any, tend_any, step_any, lw_any, lb_any, cw_any, cb_any, zf_any, yfh_any, yfl_any, xf_any,
-    sel_any, xb_any, yh_any, yl_any, tz_any, w_any, *rest,
+    kyl, kzl, oc, lag, ahead, at_xf, at_sel, at_xb, vel_any, tend_any, step_any, lw_any, lb_any, cw_any, cb_any, zf_any,
+    yf_any, ye_any, tab_any, w_any, *rest,
 ):
     chunks = LANES // (oc * (lw_any.shape[0] + 1))
     if chunks > 1:
@@ -85,9 +85,9 @@
     else:
         feats_ref = None
     (
-        dlast_ref, adv_ref, comb_ref, vel_ref, tend_ref, step_ref, lw_ref, lb_ref, cw_ref, cb_ref, zf_ref, yfh_ref,
-        yfl_ref, xf_ref, sel_ref, xb_ref, yh_ref, yl_ref, tz_ref, w_ref, lift_ref, wl_ref, wt_ref, yexp_ref, zsend, zrecv,
-        ypad, ysend, yrecv, amp_ref, xsend, xrecv, csend, crecv, in_sems, z_ss, z_rs, y_ss, y_rs, x_ss, x_rs, c_ss, c_rs,
+        dlast_ref, adv_ref, comb_ref, vel_ref, tend_ref, step_ref, lw_ref, lb_ref, cw_ref, cb_ref, zf_ref, yf_ref, ye_ref,
+        tab_ref, w_ref, lift_ref, wl_ref, wt_ref, zsend, zrecv, ypad, ysend, yrecv, amp_ref, xsend, xrecv, csend, crecv,
+        in_sems, send_sems, z_rs, y_rs, x_rs, c_rs,
     ) = rest
     rows, cols = lax.axis_size("row"), lax.axis_size("col")
     my_row, my_col = lax.axis_index("row"), lax.axis_index("col")
@@ -99,14 +99,13 @@
     slots = kyl * kzl
     modes = slots * KX
     ko = kzl * oc
+    early = 2
 
     loads = {}
     order = [
         ("vel", vel_any, vel_ref), ("tend", tend_any, tend_ref), ("step", step_any, step_ref), ("zf", zf_any, zf_ref),
         ("lw", lw_any, lw_ref), ("lb", lb_any, lb_ref), ("cw", cw_any, cw_ref), ("cb", cb_any, cb_ref),
-        ("w", w_any, w_ref), ("yfh", yfh_any, yfh_ref), ("yfl", yfl_any, yfl_ref), ("yh", yh_any, yh_ref),
-        ("yl", yl_any, yl_ref), ("xf", xf_any, xf_ref), ("sel", sel_any, sel_ref), ("xb", xb_any, xb_ref),
-        ("tz", tz_any, tz_ref),
+        ("w", w_any, w_ref), ("yf", yf_any, yf_ref), ("tab", tab_any, tab_ref), ("ye", ye_any, ye_ref),
     ]
     for n, (name, source, target) in enumerate(order):
         loads[name] = pltpu.make_async_copy(source, target, in_sems.at[n])
@@ -125,9 +124,10 @@
         pl.semaphore_signal(barrier, inc=1, device_id={"col": peer}, device_id_type=MESH)
 
     def send(source, target, sends, receives, **where):
-        copy = pltpu.make_async_remote_copy(source, target, sends, receives, device_id=where, device_id_type=MESH)
-        copy.start()
-        return copy
+        pltpu.make_async_remote_copy(source, target, sends, receives, device_id=where, device_id_type=MESH).start()
+
+    def take(ref, semaphore):
+        pltpu.make_async_copy(ref, ref, semaphore).wait()
 
     loaded("vel", "tend", "step", "zf")
     step = step_ref[0:1, 0:1]
@@ -139,9 +139,8 @@
         z = both[:freq] + both[freq:] + dot_lanes(zf_ref[0:freq, :], low)
         zsend[:, j * rk:(j + 1) * rk, :] = z.reshape(cols, rk, cells)
     pl.semaphore_wait(barrier, rows + cols - 2)
-    z_copies = [
-        send(zsend.at[peer], zrecv.at[my_col], z_ss.at[i], z_rs.at[i], col=peer) for i, peer in enumerate(col_peers)
-    ]
+    for peer in col_peers:
+        send(zsend.at[peer], zrecv.at[my_col], send_sems.at[0], z_rs, col=peer)
     zrecv[pl.ds(my_col, 1)] = zsend[pl.ds(my_col, 1)]
 
     loaded("lw", "lb", "cw", "cb")
@@ -176,37 +175,8 @@
         both = dot(w_ref[at, :], lift_ref[...])
         wl_ref[at, :] = both[:, :LANES] + both[:, LANES:]
 
-    weigh(0)
-    weigh(1)
-    loaded("yfh", "yfl")
-    for copy in z_copies:
-        copy.wait_recv()
-
-    x = jnp.concatenate([zrecv[s] for s in range(cols)], 1)
-    depth = width_in * rk
-    halves = stacked(x)
-    both = dot(halves, yfh_ref[...])
-    y = both[:depth] + both[depth:] + dot(x.astype(BF16), yfl_ref[...])
-    lanes = yfh_ref.shape[1] // 2
-    wide = ypad.shape[1]
-    parts = lanes // wide
-    slot = ypad.shape[0] // parts
-    ypad[...] = jnp.zeros_like(ypad)
-    low_rows = iota((rk, lanes), 0) < rk // 2
-    for j in range(width_in):
-        here = y[j * rk:(j + 1) * rk]
-        turned = pltpu.roll(here[:, lanes:], rk // 2, 0)
-        here = here[:, :lanes] + jnp.where(low_rows, turned, -turned)
-        for p in range(parts):
-            ypad[p * slot + j * rk:p * slot + (j + 1) * rk, :] = here[:, p * wide:(p + 1) * wide]
-    ysend[...] = jnp.transpose(ypad[...]).reshape(ysend.shape)
-    y_copies = [
-        send(ysend.at[peer], yrecv.at[my_row], y_ss.at[i], y_rs.at[i], row=peer) for i, peer in enumerate(row_peers)
-    ]
-    yrecv[pl.ds(my_row, 1)] = ysend[pl.ds(my_row, 1)]
-
-    weigh(2)
-    weigh(3)
+    for n in range(4):
+        weigh(n)
 
     def turn(n, carry):
         ri, at = n // (KX // 8), (n % (KX // 8)) * 8
@@ -225,27 +195,38 @@
             wt_ref[ri, s, pl.ds(pl.multiple_of(at, 8), 8), :] = held[s]
         return carry
 
-    lax.fori_loop(0, 2 * (KX // 8), turn, 0)
-
-    loaded("yh", "yl")
-    pairs = 2 * rows
-    a = xsend.shape[2] // 2
-    total = pairs * a
-    width = 2 * cells
-    same = iota((pairs, a, width), 1) == (iota((pairs, a, width), 2) // (cells // a)) % a
-
-    def expand(d, carry):
-        for h, table in enumerate((yh_ref, yl_ref)):
-            for l in range(kyl):
-                full = jnp.where(same, table[d, l].astype(F32)[:, None, :], 0.0)
-                yexp_ref[d, h, l * total:(l + 1) * total, :] = full.reshape(total, width).astype(BF16)
-        return carry
-
-    lax.fori_loop(0, cols, expand, 0)
-    loaded("xf", "sel", "xb", "tz")
-    for copy in y_copies:
-        copy.wait_recv()
-
+    lax.fori_loop(0, early, turn, 0)
+
+    loaded("yf")
+    take(zrecv.at[pl.ds(0, cols - 1)], z_rs)
+
+    x = jnp.concatenate([zrecv[s] for s in range(cols)], 1)
+    depth = width_in * rk
+    halves = stacked(x)
+    both = dot(halves, yf_ref[0])
+    y = both[:depth] + both[depth:] + dot(x.astype(BF16), yf_ref[1])
+    lanes = yf_ref.shape[2] // 2
+    wide = ypad.shape[1]
+    parts = lanes // wide
+    slot = ypad.shape[0] // parts
+    ypad[...] = jnp.zeros_like(ypad)
+    low_rows = iota((rk, lanes), 0) < rk // 2
+    for j in range(width_in):
+        here = y[j * rk:(j + 1) * rk]
+        turned = pltpu.roll(here[:, lanes:], rk // 2, 0)
+        here = here[:, :lanes] + jnp.where(low_rows, turned, -turned)
+        for p in range(parts):
+            ypad[p * slot + j * rk:p * slot + (j + 1) * rk, :] = here[:, p * wide:(p + 1) * wide]
+    ysend[...] = jnp.transpose(ypad[...]).reshape(ysend.shape)
+    for peer in row_peers:
+        send(ysend.at[peer], yrecv.at[my_row], send_sems.at[1], y_rs, row=peer)
+    yrecv[pl.ds(my_row, 1)] = ysend[pl.ds(my_row, 1)]
+
+    lax.fori_loop(early, 2 * (KX // 8), turn, 0)
+    loaded("tab", "ye")
+    take(yrecv.at[pl.ds(0, rows - 1)], y_rs)
+
+    a = xsend.shape[3]
     deep = yrecv.shape[1] // a
     is_re = (iota((rows * a, LANES), 1) % rk) < rk // 2
     plain, cross = [], []
@@ -255,15 +236,19 @@
         cross.append(jnp.where(is_re, pltpu.roll(u, LANES - rk // 2, 1), -pltpu.roll(u, rk // 2, 1)))
     u = jnp.concatenate([jnp.concatenate(plain, 1), jnp.concatenate(cross, 1)], 0)
     high, low = split(u)
-    both = dot(xf_ref[...], high)
-    q = both[:KX] + both[KX:] + dot(xf_ref[0:KX, :], low)
-    both = dot(stacked(q), sel_ref[...])
-    amp_ref[...] = both[:KX] + both[KX:]
+    xf = tab_ref[at_xf:at_xf + 2 * KX, :2 * rows * a]
+    both = dot(xf, high)
+    q = both[:KX] + both[KX:] + dot(xf[:KX], low)
+    halves = stacked(q)
+    for j in range(width_in):
+        both = dot(halves, tab_ref[at_sel + j * deep * LANES:at_sel + (j + 1) * deep * LANES, :])
+        amp_ref[:, 2 * j * LANES:(2 * j + 2) * LANES] = both[:KX] + both[KX:]
     origin = jnp.where((my_row == 0) & (my_col == 0), 1.0, 0.0)
     flag = jnp.where((iota((KX, LANES), 0) == 0) & (iota((KX, LANES), 1) < oc), origin, 0.0)
 
-    x_copies = []
-    for c in range(chunks):
+    xb = tab_ref[at_xb:at_xb + rows * 2 * a, :6 * KX]
+
+    def mix(c):
         pr = wt_ref[0, c * group + width_in] * flag
         pi = wt_ref[1, c * group + width_in] * flag
         for j in range(width_in):
@@ -273,61 +258,77 @@
             pr = pr + (wr * ar - wi * ai)
             pi = pi + (wr * ai + wi * ar)
         high, low = split(jnp.concatenate([pr, pi], 0))
-        xsend[c] = dot(xb_ref[...], jnp.concatenate([high, low, high], 0)).reshape(xsend.shape[1:])
-        x_copies.append([
-            send(xsend.at[c, peer], xrecv.at[c, my_row], x_ss.at[c, i], x_rs.at[c, i], row=peer)
-            for i, peer in enumerate(row_peers)
-        ])
+        xsend[c] = dot(xb, jnp.concatenate([high, low, high], 0)).reshape(xsend.shape[1:])
+        for peer in row_peers:
+            send(xsend.at[c, peer], xrecv.at[c, my_row], send_sems.at[2], x_rs.at[c], row=peer)
         xrecv[c, pl.ds(my_row, 1)] = xsend[c, pl.ds(my_row, 1)]
 
-    tz = tz_ref[...]
-    c_copies = []
+    tz = tab_ref[0:6 * KZ, :]
+    side = rows * a
+    middle = cells // 2
+    upper = iota((ko, LANES), 1) >= LANES // 2
+
+    def swap(first, second):
+        return (
+            jnp.where(upper, pltpu.roll(second, LANES // 2, 1), first),
+            jnp.where(upper, second, pltpu.roll(first, LANES // 2, 1)),
+        )
 
     def landing(c):
         return dlast_ref if c == chunks - 1 else crecv.at[c]
 
     def inverse_y(c):
-        for copy in x_copies[c]:
-            copy.wait_recv()
-        turned = jnp.transpose(xrecv[c].reshape(total, LANES))
-        held = jnp.concatenate([turned[l * ko:(l + 1) * ko] for l in range(kyl)], 1)
-        halves = stacked(held)
+        take(xrecv.at[c, pl.ds(0, rows - 1)], x_rs.at[c])
+        turned = jnp.concatenate([xrecv[c, :, h].reshape(side, LANES) for h in range(2)], 0)
+        turned = jnp.transpose(turned)
+        held = [turned[l * ko:(l + 1) * ko] for l in range(kyl)]
+        if side == LANES:
+            held = [jnp.concatenate([x[:, h * side:(h + 1) * side] for x in held], 1) for h in range(2)]
+        else:
+            tiles = [swap(held[l], held[l + 1]) for l in range(0, kyl, 2)]
+            held = [jnp.concatenate([x[h] for x in tiles], 1) for h in range(2)]
+        halves = stacked(jnp.concatenate(held, 0))
         at = pl.ds(pl.multiple_of(my_col * 2 * ko, 2 * ko), 2 * ko)
-        started = []
-        for i in list(range(1, cols)) + [0]:
-            d = lax.rem(my_col + i, cols)
-            both = dot(halves, yexp_ref[d, 0])
-            acc = both[:ko] + both[ko:] + dot(halves[:ko], yexp_ref[d, 1])
-            acc = jnp.concatenate([acc[:, v * cells:(v + 1) * cells] for v in range(2)], 0)
-            if i == 0:
-                landing(c)[at, :] = acc
-            else:
-                csend[c, i - 1] = acc
-                started.append(
-                    send(csend.at[c, i - 1], landing(c).at[at, :], c_ss.at[c, i - 1], c_rs.at[c, i - 1], col=d)
-                )
-        c_copies.append(started)
+        for i in range(0, cols, 2):
+            targets = [lax.rem(my_col + i + 1, cols), lax.rem(my_col + i + 2, cols)]
+            both = dot(halves, jnp.concatenate([ye_ref[d, 0] for d in targets], 1))
+            acc = both[:2 * ko] + both[2 * ko:]
+            acc = acc + dot(halves[:2 * ko], jnp.concatenate([ye_ref[d, 1] for d in targets], 1))
+            for n, d in enumerate(targets):
+                here = acc[:, n * LANES:(n + 1) * LANES]
+                here = jnp.concatenate(swap(here[:ko], here[ko:]), 0)
+                if i + n == cols - 1:
+                    landing(c)[at, :] = here
+                else:
+                    csend[c, i + n] = here
+                    send(csend.at[c, i + n], landing(c).at[at, :], send_sems.at[3], c_rs.at[c], col=d)
+
+    def arrive(c):
+        take(landing(c).at[pl.ds(0, (cols - 1) * 2 * ko), :], c_rs.at[c])
 
     def inverse_z(c):
-        for copy in c_copies[c]:
-            copy.wait_recv()
+        arrive(c)
         for i in range(oc):
             o = c * oc + i
             row = lambda j: comb_ref[o:o + 1, j * LANES:(j + 1) * LANES]
             d = crecv[c, pl.ds(i, cols * 2 * kzl, stride=oc), :]
             feats_ref[o] = one_channel(d, row, adv_ref, tz)
 
+    for c in range(min(ahead, chunks)):
+        mix(c)
     for c in range(chunks):
         inverse_y(c)
+        if c + ahead < chunks:
+            mix(c + ahead)
         if 0 <= c - lag < chunks - 1:
             inverse_z(c - lag)
     for c in range(max(chunks - lag, 0), chunks - 1):
         inverse_z(c)
-    for copy in c_copies[chunks - 1]:
-        copy.wait_recv()
-    for copies in [z_copies, y_copies] + x_copies + c_copies:
-        for copy in copies:
-            copy.wait_send()
+    arrive(chunks - 1)
+    take(zsend.at[pl.ds(0, cols - 1)], send_sems.at[0])
+    take(ysend.at[pl.ds(0, rows - 1)], send_sems.at[1])
+    take(xsend.at[:, pl.ds(0, rows - 1)], send_sems.at[2])
+    take(csend, send_sems.at[3])
 
 
 def finish_kernel(oc, depth, *refs):
@@ -367,7 +368,7 @@
     oc = LANES // slots
     chunks = channels // oc
     ko = kzl * oc
-    lag = 3
+    lag, ahead = 3, 3
     vmem = pl.BlockSpec(memory_space=pltpu.VMEM)
     anywhere = pl.BlockSpec(memory_space=pl.ANY)
     stored = spectral_weight.reshape(2 * modes, channels * channels)
@@ -387,7 +388,7 @@
     yf = np.stack([yc, ys], 0).reshape(2, rows, deep, parts, 1, cols, 1, b)
     yf = yf * np.eye(a).reshape(1, 1, 1, 1, a, 1, a, 1)
     yf = yf.transpose(0, 3, 1, 2, 4, 5, 6, 7).reshape(2 * parts * rows * deep * a, cols * cells).T
-    yfh, yfl = np_halves(yf)
+    yf = np.stack(np_halves(yf), 0)
     sel = np.zeros((deep, parts, slot, width_in, 2, kyl, kzl, oc), np.float32)
     for l in range(kyl):
         for j in range(width_in):
@@ -396,26 +397,29 @@
                     sel[l // parts, l % parts, j * rk + ri * (rk // 2) + k, j, ri, l, k] = 1
     sel = sel.reshape(deep * LANES, width_in * 2 * LANES)
     xb = np.stack([np.stack([xc, -xs], 0), np.stack([xs, xc], 0)], 0)
-    xb = xb.reshape(2, 2, KX, rows, a).transpose(3, 0, 4, 1, 2).reshape(rows * 2 * a, 2 * KX)
+    xb = xb.reshape(2, 2, KX, rows, 2, a // 2).transpose(3, 4, 0, 5, 1, 2).reshape(rows * 2 * a, 2 * KX)
     xbh, xbl = np_halves(xb)
     xb3 = np.concatenate([xbh, xbh, xbl], 1)
     yb = np.stack([np.stack([yc, ys], 0), np.stack([-ys, yc], 0)], 0)
     yb = yb.reshape(2, 2, rows, kyl, cols, b).transpose(4, 3, 2, 0, 1, 5)
-    yb = np.broadcast_to(yb[..., None, :], (cols, kyl, rows, 2, 2, a, b)).reshape(cols, kyl, rows * 2, 2 * cells)
-    ybh, ybl = np_halves(yb)
+    yb = yb.reshape(cols, kyl, rows, 2, 1, 2, 1, b) * np.eye(a // 2).reshape(a // 2, 1, a // 2, 1)
+    ye = np.stack(np_halves(yb.reshape(cols, kyl * rows * a, cells)), 1)
     twice = np.where(np.arange(KZ) == 0, 1.0, 2.0)[:, None]
     zb = np.stack([twice * zc, -twice * zs], 0).reshape(2, cols, kzl, nz).transpose(1, 0, 2, 3).reshape(2 * KZ, nz)
     zbh, zbl = np_halves(zb)
     zb3 = np.concatenate([zbh, zbh, zbl], 0)
     tz = jnp.asarray(zb3)
+    sel = sel.reshape(deep * LANES, width_in, 2 * LANES).transpose(1, 0, 2).reshape(-1, 2 * LANES)
+    pieces = [zb3, xf2, sel, xb3]
+    table = np.concatenate([np.pad(np.asarray(x, jnp.bfloat16), ((0, 0), (0, nz - x.shape[1]))) for x in pieces], 0)
+    starts = [zb3.shape[0], zb3.shape[0] + xf2.shape[0], zb3.shape[0] + xf2.shape[0] + sel.shape[0]]
 
     results = []
     for sample in range(samples):
         inputs = [
             velocity[sample].reshape(width_in, cells, nz), tendency[sample].reshape(width_in, cells, nz),
             step_size[sample].reshape(1, 1), lift_weight.T, lift_bias.reshape(1, channels), local_weight,
-            local_bias.reshape(1, channels), jnp.asarray(zf2), jnp.asarray(yfh), jnp.asarray(yfl), jnp.asarray(xf2),
-            jnp.asarray(sel, BF16), jnp.asarray(xb3), jnp.asarray(ybh), jnp.asarray(ybl), tz, stored,
+            local_bias.reshape(1, channels), jnp.asarray(zf2), jnp.asarray(yf), jnp.asarray(ye), jnp.asarray(table), stored,
         ]
         dma = lambda *shape: pltpu.SemaphoreType.DMA(shape)
         first = channels - oc
@@ -427,7 +431,7 @@
         if first:
             outs = [jax.ShapeDtypeStruct((first, cells, nz), BF16)] + outs
         held = pl.pallas_call(
-            functools.partial(layer_kernel, kyl, kzl, oc, lag),
+            functools.partial(layer_kernel, kyl, kzl, oc, lag, ahead, *starts),
             out_shape=outs,
             in_specs=[anywhere] * len(inputs),
             out_specs=[vmem] * len(outs),
@@ -435,20 +439,17 @@
                 pltpu.VMEM((channels * channels, 2 * LANES), BF16),
                 pltpu.VMEM((2 * modes, LANES), F32),
                 pltpu.VMEM((2, slots, KX, LANES), F32),
-                pltpu.VMEM((cols, 2, kyl * rows * 2 * a, 2 * cells), BF16),
                 pltpu.VMEM((cols, width_in * rk, cells), F32),
                 pltpu.VMEM((cols, width_in * rk, cells), F32),
                 pltpu.VMEM((parts * slot, rows * deep * a), F32),
                 pltpu.VMEM((rows, deep * a, LANES), F32),
                 pltpu.VMEM((rows, deep * a, LANES), F32),
                 pltpu.VMEM((KX, width_in * 2 * LANES), F32),
-                pltpu.VMEM((chunks, rows, 2 * a, LANES), F32),
-                pltpu.VMEM((chunks, rows, 2 * a, LANES), F32),
+                pltpu.VMEM((chunks, rows, 2, a, LANES), F32),
+                pltpu.VMEM((chunks, rows, 2, a, LANES), F32),
                 pltpu.VMEM((chunks, cols - 1, 2 * ko, cells), F32),
                 pltpu.VMEM((chunks, cols * 2 * ko, cells), F32),
-                dma(len(inputs)),
-                dma(cols - 1), dma(cols - 1), dma(rows - 1), dma(rows - 1),
-                dma(chunks, rows - 1), dma(chunks, rows - 1), dma(chunks, cols - 1), dma(chunks, cols - 1),
+                dma(len(inputs)), dma(4), pltpu.SemaphoreType.DMA, pltpu.SemaphoreType.DMA, dma(chunks), dma(chunks),
             ],
             compiler_params=pltpu.CompilerParams(
                 vmem_limit_bytes=40 * 1024 * 1024, collective_id=0, has_side_effects=True

time: 38.6 us -> 35 us (0.907)
  Pallas kernels: 37.8 us -> 34.2 us
    pallas_call x1, Pallas kernels: 36.4 us -> 32.8 us  [per_device(): pl.pallas_call(functools.partial(layer_kernel, kyl, kzl, oc, lag, ahead,...]
where the time goes in v3:
time: 35 us; the launch traced here: 34.9 us
  Pallas kernels  34.2 us (98%)
  between operations  0.68 us (2%)
    pallas_call x1, Pallas kernels, per_device(): pl.pallas_call(functools.partial(layer_kernel, kyl, kzl, oc, lag, ahead,...  32.8 us
    pallas_call x1, Pallas kernels, per_device(): pl.pallas_call(functools.partial(finish_kernel, oc, cols * 2 * kzl), out_...  1.35 us

profile of v3, /device:TPU:0, one launch (start us, length us, event | category | flops | bytes accessed | tf_op | source)
XLA Modules:
  0.0 34.9 jit_solution(5038257574590870318)
XLA Ops:
  0.7 0.0 copy-start
  0.7 32.8 %shard_map.127 = (bf16[28,128,256]{2,1,0:T(8,128)(2,1)S(1)}, f32[256,128]{1,0:T(8,128)S(1)}, f32[3,128,256]{2,1,0:T(8,128)S(1)}, f32[32,512]{1,0:T(8,128)S(1)}) custom-call(f32[3,128,256]{2,1,0:T(8,128)} %bitcast.10, f32[3,128,256]{2,1,0:T(8,128)} %bitcast.11, f32[1,1]{1,0:T(1,128)} %bitcast.8.step_any, f32[3,32]{1,0:T(4,128)} %bitcast.12, ...), custom_call_target="tpu_custom_call" | custom-call | tf_op jit(solution)/shard_map/pallas_call | solution.py:433
  33.5 0.0 copy-done
  33.5 1.3 %shard_map.128 = bf16[32,128,256]{2,1,0:T(8,128)(2,1)} custom-call(bf16[28,128,256]{2,1,0:T(8,128)(2,1)S(1)} %get-tuple-element.9.refs_0_, f32[256,128]{1,0:T(8,128)S(1)} %get-tuple-element.10.refs_1_, f32[3,128,256]{2,1,0:T(8,128)S(1)} %get-tuple-element.11.refs_2_, f32[32,512]{1,0:T(8,128)S(1)} %get-tuple-element.12.refs_3_, bf16[192,256]{1,0:T(8,128)(2,1)S(1)} %copy-done), custom_call_target="tpu_custom_call" | custom-call | tf_op jit(solution)/shard_map/pallas_call | solution.py:458
Async XLA Ops:
  0.7 32.9 %copy-start = (bf16[192,256]{1,0:T(8,128)(2,1)S(1)}, bf16[192,256]{1,0:T(8,128)(2,1)}, u32[]{:S(2)}) copy-start(bf16[192,256]{1,0:T(8,128)(2,1)} %constant.10.clone.refs_4_) | copy-start | bytes 294916

commit v4 on v3

--- a/solution.py
+++ b/solution.py
@@ -368,7 +368,7 @@
     oc = LANES // slots
     chunks = channels // oc
     ko = kzl * oc
-    lag, ahead = 3, 3
+    lag, ahead = 3, 4
     vmem = pl.BlockSpec(memory_space=pltpu.VMEM)
     anywhere = pl.BlockSpec(memory_space=pl.ANY)
     stored = spectral_weight.reshape(2 * modes, channels * channels)

time: 35 us -> 34.1 us (0.974)
  Pallas kernels: 34.2 us -> 33.3 us
    pallas_call x1, Pallas kernels: 32.8 us -> 32 us  [per_device(): pl.pallas_call(functools.partial(layer_kernel, kyl, kzl, oc, lag, ahead,...]
where the time goes in v4:
time: 34.1 us; the launch traced here: 34 us
  Pallas kernels  33.3 us (98%)
  between operations  0.68 us (2%)
    pallas_call x1, Pallas kernels, per_device(): pl.pallas_call(functools.partial(layer_kernel, kyl, kzl, oc, lag, ahead,...  32 us
    pallas_call x1, Pallas kernels, per_device(): pl.pallas_call(functools.partial(finish_kernel, oc, cols * 2 * kzl), out_...  1.35 us

profile of v4, /device:TPU:0, one launch (start us, length us, event | category | flops | bytes accessed | tf_op | source)
XLA Modules:
  0.0 34.0 jit_solution(1807620352003826656)
XLA Ops:
  0.7 0.0 copy-start
  0.7 32.0 %shard_map.127 = (bf16[28,128,256]{2,1,0:T(8,128)(2,1)S(1)}, f32[256,128]{1,0:T(8,128)S(1)}, f32[3,128,256]{2,1,0:T(8,128)S(1)}, f32[32,512]{1,0:T(8,128)S(1)}) custom-call(f32[3,128,256]{2,1,0:T(8,128)} %bitcast.10, f32[3,128,256]{2,1,0:T(8,128)} %bitcast.11, f32[1,1]{1,0:T(1,128)} %bitcast.8.step_any, f32[3,32]{1,0:T(4,128)} %bitcast.12, ...), custom_call_target="tpu_custom_call" | custom-call | tf_op jit(solution)/shard_map/pallas_call | solution.py:433
  32.6 0.0 copy-done
  32.6 1.3 %shard_map.128 = bf16[32,128,256]{2,1,0:T(8,128)(2,1)} custom-call(bf16[28,128,256]{2,1,0:T(8,128)(2,1)S(1)} %get-tuple-element.9.refs_0_, f32[256,128]{1,0:T(8,128)S(1)} %get-tuple-element.10.refs_1_, f32[3,128,256]{2,1,0:T(8,128)S(1)} %get-tuple-element.11.refs_2_, f32[32,512]{1,0:T(8,128)S(1)} %get-tuple-element.12.refs_3_, bf16[192,256]{1,0:T(8,128)(2,1)S(1)} %copy-done), custom_call_target="tpu_custom_call" | custom-call | tf_op jit(solution)/shard_map/pallas_call | solution.py:458
Async XLA Ops:
  0.7 32.0 %copy-start = (bf16[192,256]{1,0:T(8,128)(2,1)S(1)}, bf16[192,256]{1,0:T(8,128)(2,1)}, u32[]{:S(2)}) copy-start(bf16[192,256]{1,0:T(8,128)(2,1)} %constant.10.clone.refs_4_) | copy-start | bytes 294916

commit v5 on v4

--- a/solution.py
+++ b/solution.py
@@ -99,7 +99,7 @@
     slots = kyl * kzl
     modes = slots * KX
     ko = kzl * oc
-    early = 2
+    early = 4
 
     loads = {}
     order = [
@@ -129,6 +129,11 @@
     def take(ref, semaphore):
         pltpu.make_async_copy(ref, ref, semaphore).wait()
 
+    def send_z(j):
+        at = pl.ds(j * rk, rk)
+        for peer in col_peers:
+            send(zsend.at[peer, at], zrecv.at[my_col, at], send_sems.at[0], z_rs, col=peer)
+
     loaded("vel", "tend", "step", "zf")
     step = step_ref[0:1, 0:1]
     for j in range(width_in):
@@ -138,9 +143,9 @@
         both = dot_lanes(zf_ref[...], high)
         z = both[:freq] + both[freq:] + dot_lanes(zf_ref[0:freq, :], low)
         zsend[:, j * rk:(j + 1) * rk, :] = z.reshape(cols, rk, cells)
-    pl.semaphore_wait(barrier, rows + cols - 2)
-    for peer in col_peers:
-        send(zsend.at[peer], zrecv.at[my_col], send_sems.at[0], z_rs, col=peer)
+        if j == 0:
+            pl.semaphore_wait(barrier, rows + cols - 2)
+        send_z(j)
     zrecv[pl.ds(my_col, 1)] = zsend[pl.ds(my_col, 1)]
 
     loaded("lw", "lb", "cw", "cb")
@@ -181,16 +186,15 @@
     def turn(n, carry):
         ri, at = n // (KX // 8), (n % (KX // 8)) * 8
         held = [wl_ref[pl.ds(pl.multiple_of(ri * modes + s * KX + at, 8), 8), :] for s in range(slots)]
+        held = [pltpu.roll(x, s * oc, 1) if s else x for s, x in enumerate(held)]
+        held = [held[-s % slots] for s in range(slots)]
         place = iota((8, LANES), 1) // oc
         bit = 1
         while bit < slots:
             upper = (place // bit) % 2 == 1
-            for s in range(slots):
-                if not s & bit:
-                    a, b = held[s], held[s | bit]
-                    held[s] = jnp.where(upper, pltpu.roll(b, bit * oc, 1), a)
-                    held[s | bit] = jnp.where(upper, b, pltpu.roll(a, LANES - bit * oc, 1))
+            held = [jnp.where(upper, held[(s - bit) % slots], held[s]) for s in range(slots)]
             bit *= 2
+        held = [pltpu.roll(x, LANES - s * oc, 1) if s else x for s, x in enumerate(held)]
         for s in range(slots):
             wt_ref[ri, s, pl.ds(pl.multiple_of(at, 8), 8), :] = held[s]
         return carry

time: 34.1 us -> 34 us (level)
  no operation moved by 1% of the time
where the time goes in v5:
time: 34 us; the launch traced here: 33.9 us
  Pallas kernels  33.2 us (98%)
  between operations  0.68 us (2%)
    pallas_call x1, Pallas kernels, per_device(): pl.pallas_call(functools.partial(layer_kernel, kyl, kzl, oc, lag, ahead,...  31.8 us
    pallas_call x1, Pallas kernels, per_device(): pl.pallas_call(functools.partial(finish_kernel, oc, cols * 2 * kzl), out_...  1.35 us

profile of v5, /device:TPU:0, one launch (start us, length us, event | category | flops | bytes accessed | tf_op | source)
XLA Modules:
  0.0 33.9 jit_solution(14654693190821361975)
XLA Ops:
  0.7 0.0 copy-start
  0.7 31.8 %shard_map.127 = (bf16[28,128,256]{2,1,0:T(8,128)(2,1)S(1)}, f32[256,128]{1,0:T(8,128)S(1)}, f32[3,128,256]{2,1,0:T(8,128)S(1)}, f32[32,512]{1,0:T(8,128)S(1)}) custom-call(f32[3,128,256]{2,1,0:T(8,128)} %bitcast.10, f32[3,128,256]{2,1,0:T(8,128)} %bitcast.11, f32[1,1]{1,0:T(1,128)} %bitcast.8.step_any, f32[3,32]{1,0:T(4,128)} %bitcast.12, ...), custom_call_target="tpu_custom_call" | custom-call | tf_op jit(solution)/shard_map/pallas_call | solution.py:437
  32.5 0.0 copy-done
  32.5 1.3 %shard_map.128 = bf16[32,128,256]{2,1,0:T(8,128)(2,1)} custom-call(bf16[28,128,256]{2,1,0:T(8,128)(2,1)S(1)} %get-tuple-element.9.refs_0_, f32[256,128]{1,0:T(8,128)S(1)} %get-tuple-element.10.refs_1_, f32[3,128,256]{2,1,0:T(8,128)S(1)} %get-tuple-element.11.refs_2_, f32[32,512]{1,0:T(8,128)S(1)} %get-tuple-element.12.refs_3_, bf16[192,256]{1,0:T(8,128)(2,1)S(1)} %copy-done), custom_call_target="tpu_custom_call" | custom-call | tf_op jit(solution)/shard_map/pallas_call | solution.py:462
Async XLA Ops:
  0.7 31.9 %copy-start = (bf16[192,256]{1,0:T(8,128)(2,1)S(1)}, bf16[192,256]{1,0:T(8,128)(2,1)}, u32[]{:S(2)}) copy-start(bf16[192,256]{1,0:T(8,128)(2,1)} %constant.10.clone.refs_4_) | copy-start | bytes 294916

commit v6 on v5

--- a/solution.py
+++ b/solution.py
@@ -318,12 +318,13 @@
             d = crecv[c, pl.ds(i, cols * 2 * kzl, stride=oc), :]
             feats_ref[o] = one_channel(d, row, adv_ref, tz)
 
-    for c in range(min(ahead, chunks)):
-        mix(c)
+    mixed = 0
     for c in range(chunks):
+        upto = min(ahead[min(c, len(ahead) - 1)], chunks)
+        for n in range(mixed, upto):
+            mix(n)
+        mixed = max(mixed, upto)
         inverse_y(c)
-        if c + ahead < chunks:
-            mix(c + ahead)
         if 0 <= c - lag < chunks - 1:
             inverse_z(c - lag)
     for c in range(max(chunks - lag, 0), chunks - 1):
@@ -372,7 +373,7 @@
     oc = LANES // slots
     chunks = channels // oc
     ko = kzl * oc
-    lag, ahead = 3, 4
+    lag, ahead = 5, (4, 5, 6, 7, 8)
     vmem = pl.BlockSpec(memory_space=pltpu.VMEM)
     anywhere = pl.BlockSpec(memory_space=pl.ANY)
     stored = spectral_weight.reshape(2 * modes, channels * channels)

time: 34 us -> 34 us (level)
  no operation moved by 1% of the time
where the time goes in v6:
time: 34 us; the launch traced here: 33.9 us
  Pallas kernels  33.2 us (98%)
  between operations  0.68 us (2%)
    pallas_call x1, Pallas kernels, per_device(): pl.pallas_call(functools.partial(layer_kernel, kyl, kzl, oc, lag, ahead,...  31.8 us
    pallas_call x1, Pallas kernels, per_device(): pl.pallas_call(functools.partial(finish_kernel, oc, cols * 2 * kzl), out_...  1.35 us

profile of v6, /device:TPU:0, one launch (start us, length us, event | category | flops | bytes accessed | tf_op | source)
XLA Modules:
  0.0 33.9 jit_solution(10193401862812778804)
XLA Ops:
  0.7 0.0 copy-start
  0.7 31.8 %shard_map.127 = (bf16[28,128,256]{2,1,0:T(8,128)(2,1)S(1)}, f32[256,128]{1,0:T(8,128)S(1)}, f32[3,128,256]{2,1,0:T(8,128)S(1)}, f32[32,512]{1,0:T(8,128)S(1)}) custom-call(f32[3,128,256]{2,1,0:T(8,128)} %bitcast.10, f32[3,128,256]{2,1,0:T(8,128)} %bitcast.11, f32[1,1]{1,0:T(1,128)} %bitcast.8.step_any, f32[3,32]{1,0:T(4,128)} %bitcast.12, ...), custom_call_target="tpu_custom_call" | custom-call | tf_op jit(solution)/shard_map/pallas_call | solution.py:438
  32.5 0.0 copy-done
  32.5 1.3 %shard_map.128 = bf16[32,128,256]{2,1,0:T(8,128)(2,1)} custom-call(bf16[28,128,256]{2,1,0:T(8,128)(2,1)S(1)} %get-tuple-element.9.refs_0_, f32[256,128]{1,0:T(8,128)S(1)} %get-tuple-element.10.refs_1_, f32[3,128,256]{2,1,0:T(8,128)S(1)} %get-tuple-element.11.refs_2_, f32[32,512]{1,0:T(8,128)S(1)} %get-tuple-element.12.refs_3_, bf16[192,256]{1,0:T(8,128)(2,1)S(1)} %copy-done), custom_call_target="tpu_custom_call" | custom-call | tf_op jit(solution)/shard_map/pallas_call | solution.py:463
Async XLA Ops:
  0.7 31.9 %copy-start = (bf16[192,256]{1,0:T(8,128)(2,1)S(1)}, bf16[192,256]{1,0:T(8,128)(2,1)}, u32[]{:S(2)}) copy-start(bf16[192,256]{1,0:T(8,128)(2,1)} %constant.10.clone.refs_4_) | copy-start | bytes 294916

commit v7 on v6

--- a/solution.py
+++ b/solution.py
@@ -101,6 +101,15 @@
     ko = kzl * oc
     early = 4
 
+    barrier = pltpu.get_barrier_semaphore()
+    row_peers = [lax.rem(my_row + i, rows) for i in range(1, rows)]
+    col_peers = [lax.rem(my_col + i, cols) for i in range(1, cols)]
+    def greet():
+      for peer in row_peers:
+          pl.semaphore_signal(barrier, inc=1, device_id={"row": peer}, device_id_type=MESH)
+      for peer in col_peers:
+          pl.semaphore_signal(barrier, inc=1, device_id={"col": peer}, device_id_type=MESH)
+
     loads = {}
     order = [
         ("vel", vel_any, vel_ref), ("tend", tend_any, tend_ref), ("step", step_any, step_ref), ("zf", zf_any, zf_ref),
@@ -110,18 +119,12 @@
     for n, (name, source, target) in enumerate(order):
         loads[name] = pltpu.make_async_copy(source, target, in_sems.at[n])
         loads[name].start()
+        if name == "step":
+            greet()
 
     def loaded(*names):
         for name in names:
             loads[name].wait()
-
-    barrier = pltpu.get_barrier_semaphore()
-    row_peers = [lax.rem(my_row + i, rows) for i in range(1, rows)]
-    col_peers = [lax.rem(my_col + i, cols) for i in range(1, cols)]
-    for peer in row_peers:
-        pl.semaphore_signal(barrier, inc=1, device_id={"row": peer}, device_id_type=MESH)
-    for peer in col_peers:
-        pl.semaphore_signal(barrier, inc=1, device_id={"col": peer}, device_id_type=MESH)
 
     def send(source, target, sends, receives, **where):
         pltpu.make_async_remote_copy(source, target, sends, receives, device_id=where, device_id_type=MESH).start()

time: 34 us -> 34 us (level)
  no operation moved by 1% of the time
where the time goes in v7:
time: 34 us; the launch traced here: 33.9 us
  Pallas kernels  33.2 us (98%)
  between operations  0.68 us (2%)
    pallas_call x1, Pallas kernels, per_device(): pl.pallas_call(functools.partial(layer_kernel, kyl, kzl, oc, lag, ahead,...  31.8 us
    pallas_call x1, Pallas kernels, per_device(): pl.pallas_call(functools.partial(finish_kernel, oc, cols * 2 * kzl), out_...  1.35 us

profile of v7, /device:TPU:0, one launch (start us, length us, event | category | flops | bytes accessed | tf_op | source)
XLA Modules:
  0.0 33.9 jit_solution(1846124682423162136)
XLA Ops:
  0.7 0.0 copy-start
  0.7 31.8 %shard_map.127 = (bf16[28,128,256]{2,1,0:T(8,128)(2,1)S(1)}, f32[256,128]{1,0:T(8,128)S(1)}, f32[3,128,256]{2,1,0:T(8,128)S(1)}, f32[32,512]{1,0:T(8,128)S(1)}) custom-call(f32[3,128,256]{2,1,0:T(8,128)} %bitcast.10, f32[3,128,256]{2,1,0:T(8,128)} %bitcast.11, f32[1,1]{1,0:T(1,128)} %bitcast.8.step_any, f32[3,32]{1,0:T(4,128)} %bitcast.12, ...), custom_call_target="tpu_custom_call" | custom-call | tf_op jit(solution)/shard_map/pallas_call | solution.py:441
  32.5 0.0 copy-done
  32.5 1.3 %shard_map.128 = bf16[32,128,256]{2,1,0:T(8,128)(2,1)} custom-call(bf16[28,128,256]{2,1,0:T(8,128)(2,1)S(1)} %get-tuple-element.9.refs_0_, f32[256,128]{1,0:T(8,128)S(1)} %get-tuple-element.10.refs_1_, f32[3,128,256]{2,1,0:T(8,128)S(1)} %get-tuple-element.11.refs_2_, f32[32,512]{1,0:T(8,128)S(1)} %get-tuple-element.12.refs_3_, bf16[192,256]{1,0:T(8,128)(2,1)S(1)} %copy-done), custom_call_target="tpu_custom_call" | custom-call | tf_op jit(solution)/shard_map/pallas_call | solution.py:466
Async XLA Ops:
  0.7 31.8 %copy-start = (bf16[192,256]{1,0:T(8,128)(2,1)S(1)}, bf16[192,256]{1,0:T(8,128)(2,1)}, u32[]{:S(2)}) copy-start(bf16[192,256]{1,0:T(8,128)(2,1)} %constant.10.clone.refs_4_) | copy-start | bytes 294916
